TPU v7x, 128 devices: a whole 4x4x4 slice. The times are simulated.
128 devices in a mesh: ga: 16 (over x, z_hi, core), ba: 8 (over y, z_lo).
Axes of the slice: x: 4, y: 4, z: 4 (z_hi: 2, z_lo: 2; z = z_hi * 2 + z_lo), core: 2. Of those that a mesh axis runs over, the one named last changes fastest.
Arguments:
- psi: float32 [2, 32768, 2048], P(None, 'ga', 'ba'), may hold values from -0.15625 to 0.15625
- dpsi: float32 [2, 32768, 512], P(None, 'ga', 'ba'), may hold values from -6 to 6
- band_weight: float32 [2048], replicated, may hold values from 0.25 to 1
- panel_band: int32 [16], P('ba'), may hold values from 0 to 15, each once
- slab_offset: int32 [16], replicated, may hold values from 0 to 2047
Outputs:
- projected: float32 [2, 32768, 512], P(None, 'ga', 'ba')
Inputs may be any that keep to these rules, and one draw needn't show every extreme that they name: panel_band is a permutation of the panel numbers.
All inputs are finite; a program needn't handle non-finite values.
Results may differ from a plain program's by a relative error of at most 0.00012.
Values sent between devices are 32-bit elements; how exact they have to be, the bound alone decides.
No kernel may reach another device: no remote copies, remote signals or barrier semaphores. Data moves between devices by JAX's collectives and lax.ppermute only.
A program may use at most 128 MiB of HBM per device.

v0:
```python
import jax
import jax.numpy as jnp
from jax import lax
from jax.experimental import pallas as pl
from jax.experimental.pallas import tpu as pltpu
from jax.sharding import Mesh
from jax.sharding import PartitionSpec as P


PANEL = 128
AXES = ("x", "zh", "c", "y", "zl")
REDUCE = ("x", "zh")
SPREAD = ("zl", "x", "zh")
CHUNKS = 4
F32 = jnp.float32


def shifted(value, axis, step):
    n = lax.axis_size(axis)
    return lax.ppermute(value, axis, [(i, (i + step) % n) for i in range(n)])


def traded(value, axes):
    return lax.all_to_all(value, axes, 0, 0, tiled=True)


def everyone(value, axes):
    return traded(jnp.broadcast_to(value[None], (lax.axis_size(axes), *value.shape)), axes)


def split(value):
    high = value.astype(jnp.bfloat16)
    low = (value - high.astype(F32)).astype(jnp.bfloat16)
    return high, low


def dot3(left, right, dims):
    (lh, ll), (rh, rl) = left, right

    def dot(a, b):
        return lax.dot_general(a, b, (dims, ((), ())), preferred_element_type=F32)

    return dot(lh, rh) + (dot(lh, rl) + dot(ll, rh))


def turned(value, block):
    half = block // 2
    pieces = []
    for k in range(0, value.shape[0], block):
        pieces += [value[k + half : k + block], -value[k : k + half]]
    return jnp.concatenate(pieces, axis=0)


def whole(value):
    zeros = (0,) * value.ndim
    return pl.BlockSpec(value.shape, lambda i, s: zeros)


def call(kernel, place, args, in_specs, out_shapes, flops=0):
    outs = [jax.ShapeDtypeStruct(s, d) for s, d in out_shapes]
    cost = pl.CostEstimate(flops=flops, bytes_accessed=0, transcendentals=0)
    return pl.pallas_call(
        kernel,
        grid_spec=pltpu.PrefetchScalarGridSpec(
            num_scalar_prefetch=1,
            grid=(1,),
            in_specs=in_specs,
            out_specs=[whole(o) for o in outs],
        ),
        out_shape=outs,
        cost_estimate=cost if flops else None,
    )(place, *args)


def roll_kernel(place, stored, mine, other):
    rows = stored.shape[1]
    lined = pltpu.roll(stored[...], place[2], 1)
    mine[...] = lined[:, : rows // 2]
    other[...] = lined[:, rows // 2 :]


def finish_kernel(place, stored, p0, q0, r0, away, out):
    home = p0[...] + (q0[...] + r0[...])
    ring = jnp.concatenate([home, away[...]], axis=1)
    out[...] = stored[...] - pltpu.roll(ring, place[3], 1)


def lined_up(place, blocks):
    own = jnp.concatenate([ref[...] for ref in blocks[:5]], axis=0)
    pair = jnp.concatenate([ref[...] for ref in blocks[5:]], axis=0)
    first = place[0] == 0
    low, high = jnp.where(first, own, pair), jnp.where(first, pair, own)
    return jnp.concatenate([low, high], axis=0)


def put(place, total, cols, keep, send):
    bands = total.shape[1]
    left, right = total[:, : bands // 2], total[:, bands // 2 :]
    first = place[1] == 0
    shards, blocks, rows = keep.shape[:3]
    for ref, value in ((keep, jnp.where(first, left, right)), (send, jnp.where(first, right, left))):
        for b in range(blocks):
            for s in range(shards):
                at = b * cols + s * rows
                ref[s, b] = value[at : at + rows]


def own_kernel(place, psi, *refs):
    blocks, (keep, send) = refs[:-2], refs[-2:]
    cols = blocks[0].shape[0]
    left = split(lined_up(place, blocks))
    right = split(jnp.concatenate([psi[0], psi[1]], axis=1))
    both = dot3(left, right, ((1,), (0,)))
    bands = both.shape[1] // 2
    put(place, both[:, :bands] + turned(both[:, bands:], cols), cols, keep, send)


def pair_kernel(place, re0, re1, im0, *refs):
    blocks, out = refs[:-1], refs[-1]
    cols, part = blocks[0].shape[0], im0.shape[0]
    left = split(lined_up(place, blocks))
    real = split(jnp.concatenate([re0[...], re1[...]], axis=0))
    total = dot3(left, real, ((1,), (0,)))
    left = tuple(v[:, :part] for v in left)
    out[...] = total + turned(dot3(left, split(im0[...]), ((1,), (0,))), cols)


def last_kernel(place, im1, before, *refs):
    blocks, (keep, send) = refs[:-2], refs[-2:]
    cols = blocks[0].shape[0]
    left = split(lined_up(place, blocks))
    total = turned(dot3(left, split(im1[...]), ((1,), (0,))), cols)
    put(place, before[...] + total, cols, keep, send)


def ready_kernel(place, psi, re0, re1, im0, im1, high, low):
    real = jnp.concatenate([re0[...], re1[...]], axis=0)
    imag = jnp.concatenate([im0[...], im1[...]], axis=0)
    value = jnp.concatenate([psi[0], psi[1], real, imag], axis=1)
    high[...], low[...] = split(value)


def weights(place, mine, other, half, r, count):
    def gathered(ref, which):
        v = ref[which]
        shards, rows = v.shape[0], v.shape[-2]
        tiles = [v[s, half, k] for k in range(r, r + count) for s in range(shards)]
        return jnp.concatenate(tiles, axis=0), shards * rows

    first = place[1] == 0
    out = []
    for which in (0, 1):
        a, cols = gathered(mine, which)
        b, _ = gathered(other, which)
        out.append(jnp.concatenate([jnp.where(first, a, b), jnp.where(first, b, a)], axis=1))
    zero = place[0] == 0
    own, pair = jnp.where(zero, out[0], out[1]), jnp.where(zero, out[1], out[0])
    return jnp.concatenate([own, -turned(own, cols), pair, -turned(pair, cols)], axis=1)


def far_kernel(place, high, low, mine, other, to_a, to_b):
    left = split(weights(place, mine, other, 0, 0, 1))
    out = dot3(left, (high[...], low[...]), ((1,), (1,)))
    half = out.shape[0] // 2
    to_a[...], to_b[...] = out[:half], out[half:]


def near_kernel(place, high, low, mine, other, up, down, p0, to_next, to_prev):
    left = split(weights(place, mine, other, 0, 0, 3))
    out = dot3(left, (high[...], low[...]), ((1,), (1,)))
    cols = p0.shape[0]
    half = cols // 2
    p0[...] = out[:cols]
    to_next[:half] = out[cols : cols + half] + up[...]
    to_next[half:] = out[cols + half : 2 * cols]
    to_prev[:half] = out[2 * cols : 2 * cols + half]
    to_prev[half:] = out[2 * cols + half :] + down[...]


def gather_y(block):
    half = block.shape[0] // 2
    before = shifted(block, "y", 1)
    after = shifted(block, "y", -1)
    far_a = shifted(before[:half], "y", 1)
    far_b = shifted(after[half:], "y", -1)
    return [block, after, far_a, far_b, before]


def per_device(psi, dpsi, band_weight, panel_band, slab_offset):
    zl, core = lax.axis_index("zl"), lax.axis_index("c")
    rows, nb = psi.shape[1:]
    half, cols = rows // 2, 2 * dpsi.shape[2]
    part = 2 * half // CHUNKS
    turn = slab_offset[lax.axis_index(("x", "zh", "c"))] + zl * half
    place = jnp.stack([zl, core, (2 * rows - turn) % rows, turn % rows]).astype(jnp.int32)
    stored = dpsi.swapaxes(1, 2).reshape(cols, rows)
    psi_spec = pl.BlockSpec((2, half, nb), lambda i, s: (0, s[0], 0))

    pieces = []
    for k in range(CHUNKS):
        plane, at = divmod(k * part, half)
        start = (plane, (1 - zl) * half + at, 0)
        piece = lax.dynamic_slice(psi, start, (1, part, nb))[0]
        pieces.append(shifted(piece, "zl", 1))
    mine, other = call(roll_kernel, place, [stored], [whole(stored)], [((cols, half), F32)] * 2)
    pair = shifted(other, "zl", 1)
    blocks = gather_y(mine) + gather_y(pair)

    shards = lax.axis_size(REDUCE)
    mac = 6 * 8 * cols * half
    out = [((shards, 8, cols // shards, nb // 2), F32)] * 2
    specs = [whole(b) for b in blocks]
    keep, send = call(own_kernel, place, [psi, *blocks], [psi_spec, *specs], out, mac * 2 * nb)
    over_c = keep + shifted(send, "c", 1)
    own_sum = traded(over_c, REDUCE).sum(0)

    early = pieces[:3]
    partial = call(
        pair_kernel,
        place,
        [*early, *blocks],
        [*map(whole, early), *specs],
        [((8 * cols, nb), F32)],
        mac * nb * 3 // 2,
    )[0]
    late = [pl.BlockSpec((b.shape[0], part), lambda i, s: (0, 1)) for b in blocks]
    keep, send = call(
        last_kernel,
        place,
        [pieces[3], partial, *blocks],
        [whole(pieces[3]), whole(partial), *late],
        out,
        mac * nb // 2,
    )
    over_c = keep + shifted(send, "c", 1)
    pair_sum = traded(over_c, REDUCE).sum(0)
    total = own_sum + shifted(pair_sum, "zl", 1)
    weight = lax.dynamic_slice_in_dim(band_weight, panel_band[core] * PANEL, PANEL)
    weighted = (total * weight).reshape(2, 4, cols // shards, nb // 2)

    high, low = call(
        ready_kernel,
        place,
        [psi, *pieces],
        [psi_spec, *map(whole, pieces)],
        [((half, 4 * nb), jnp.bfloat16)] * 2,
        mac,
    )
    far = weighted[:, 2:3]
    near = jnp.concatenate([weighted[:, :2], weighted[:, 3:]], axis=1)
    far_mine = everyone(far, SPREAD)
    far_mine = far_mine.reshape(2, shards, *far.shape)
    far_other = shifted(far_mine, "c", 1)
    near_mine = everyone(near, SPREAD)
    near_mine = near_mine.reshape(2, shards, *near.shape)
    near_other = shifted(near_mine, "c", 1)

    def of_half(value, which):
        def index(i, s):
            return (0, 0, 1 - s[0] if which else s[0], 0, 0, 0)

        return pl.BlockSpec((2, shards, 1, *value.shape[3:]), index)

    steps = []
    for which in (1, 0):
        args = [high, low, far_mine, far_other]
        specs = [whole(high), whole(low), *[of_half(far_mine, which)] * 2]
        shapes = [((cols // 2, half), F32)] * 2
        a, b = call(far_kernel, place, args, specs, shapes, mac * nb // 2)
        steps.append((shifted(a, "y", 1), shifted(b, "y", -1)))
    results = []
    for which in (1, 0):
        up, down = steps[1 - which]
        args = [high, low, near_mine, near_other, up, down]
        specs = [whole(high), whole(low), *[of_half(near_mine, which)] * 2, whole(up), whole(down)]
        shapes = [((cols, half), F32)] * 3
        p0, to_next, to_prev = call(near_kernel, place, args, specs, shapes, mac * nb * 3 // 2)
        q0 = shifted(to_next, "y", 1)
        r0 = shifted(to_prev, "y", -1)
        results.append((p0, q0, r0))
    p0, q0, r0 = results[0]
    away = shifted(p0 + (q0 + r0), "zl", 1)
    args = [stored, *results[1], away]
    done = call(finish_kernel, place, args, [whole(a) for a in args], [(stored.shape, F32)])[0]
    return done.reshape(2, cols // 2, rows).swapaxes(1, 2)


def solution(mesh):
    fine = Mesh(mesh.devices.reshape(4, 2, 2, 4, 2), AXES)
    ga, ba = ("x", "zh", "c"), ("y", "zl")
    in_specs = (P(None, ga, ba), P(None, ga, ba), P(), P(ba), P())

    return jax.shard_map(
        per_device, mesh=fine, in_specs=in_specs, out_specs=P(None, ga, ba), check_vma=False
    )
```

profile of v0, /device:TPU:0, one launch (start us, length us, event | category | flops | bytes accessed | tf_op | source)
XLA Modules:
  0.0 236.1 jit_solution(7971484609035835077)
XLA Ops:
  2.5 3.3 %shard_map.56 = (f32[128,1024]{1,0:T(8,128)}, f32[128,1024]{1,0:T(8,128)}) custom-call(s32[4]{0:T(128)} %pad_add_fusion.place, f32[128,2048]{1,0:T(8,128)} %bitcast.25), custom_call_target="tpu_custom_call" | custom-call | tf_op jit(solution)/shard_map/pallas_call | solution.py:62
  5.8 2.0 collective-permute-start.8
  11.1 9.0 %collective-permute-done.8.refs_5_ = f32[128,1024]{1,0:T(8,128)} collective-permute-done((f32[128,1024]{1,0:T(8,128)}, f32[128,1024]{1,0:T(8,128)}, u32[]{:S(2)}, u32[]{:S(2)}) %collective-permute-start.8) | collective-permute-done | bytes 524320 | tf_op jit(solution)/shard_map/ppermute | solution.py:20
  21.7 2.4 %dynamic-slice_bitcast_fusion = (f32[512,256]{1,0:T(8,128)}, f32[512,256]{1,0:T(8,128)S(1)}, f32[512,256]{1,0:T(8,128)S(1)}, f32[512,256]{1,0:T(8,128)S(1)}) fusion(f32[2,2048,256]{2,1,0:T(8,128)} %psi.3, s32[]{:T(128)S(6)} %select_n.32, s32[]{:T(128)S(6)} %select_n.31), kind=kLoop, calls=%fused_computation.1 | loop fusion | bytes 4194312 | tf_op jit(solution)/shard_map/squeeze | solution.py:203
  29.5 5.1 %collective-permute-done.10.refs_9_ = f32[128,1024]{1,0:T(8,128)S(1)} collective-permute-done((f32[128,1024]{1,0:T(8,128)}, f32[128,1024]{1,0:T(8,128)S(1)}, u32[]{:S(2)}, u32[]{:S(2)}) %collective-permute-start.10) | collective-permute-done | bytes 524320 | tf_op jit(solution)/shard_map/ppermute | solution.py:20
  38.6 1.9 collective-permute-done.re0
  42.4 9.5 %collective-permute-done.1.re1 = f32[512,256]{1,0:T(8,128)} collective-permute-done((f32[512,256]{1,0:T(8,128)S(1)}, f32[512,256]{1,0:T(8,128)}, u32[]{:S(2)}, u32[]{:S(2)}) %collective-permute-start.1) | collective-permute-done | bytes 524320 | tf_op jit(solution)/shard_map/ppermute | solution.py:20
  52.3 10.9 %collective-permute-done.2.im0 = f32[512,256]{1,0:T(8,128)} collective-permute-done((f32[512,256]{1,0:T(8,128)S(1)}, f32[512,256]{1,0:T(8,128)}, u32[]{:S(2)}, u32[]{:S(2)}) %collective-permute-start.2) | collective-permute-done | bytes 524320 | tf_op jit(solution)/shard_map/ppermute | solution.py:20
  65.0 4.7 %collective-permute-done.12.refs_8_ = f32[64,1024]{1,0:T(8,128)} collective-permute-done((f32[64,1024]{1,0:T(8,128)S(1)}, f32[64,1024]{1,0:T(8,128)}, u32[]{:S(2)}, u32[]{:S(2)}) %collective-permute-start.12) | collective-permute-done | bytes 262176 | tf_op jit(solution)/shard_map/ppermute | solution.py:20
  69.6 6.9 %shard_map.58.before = f32[1024,256]{1,0:T(8,128)} custom-call(s32[4]{0:T(128)} %pad_add_fusion.place, f32[512,256]{1,0:T(8,128)} %copy-done.8, f32[512,256]{1,0:T(8,128)} %collective-permute-done.1.re1, f32[512,256]{1,0:T(8,128)} %collective-permute-done.2.im0, f32[128,1024]{1,0:T(8,128)} %get-tuple-element.25.refs_0_, f32[128,1024]{1,0:T(8,128)} %copy-done.3, ...), custom_call_target="tpu_custom_call" | custom-call | flops 2415919104 | tf_op jit(solution)/shard_map/pallas_call | solution.py:62
  77.3 4.6 %shard_map.59 = (f32[8,8,16,128]{3,2,1,0:T(8,128)}, f32[8,8,16,128]{3,2,1,0:T(8,128)}) custom-call(s32[4]{0:T(128)} %pad_add_fusion.place, f32[512,256]{1,0:T(8,128)} %copy-done.1, f32[1024,256]{1,0:T(8,128)} %shard_map.58.before, f32[128,1024]{1,0:T(8,128)} %get-tuple-element.25.refs_0_, f32[128,1024]{1,0:T(8,128)} %copy-done.3, f32[64,1024]{1,0:T(8,128)} %copy-done.14, ...), custom_call_target="tpu_custom_call" | custom-call | flops 805306368 | tf_op jit(solution)/shard_map/pallas_call | solution.py:62
  82.0 8.0 %shard_map.57 = (f32[8,8,16,128]{3,2,1,0:T(8,128)}, f32[8,8,16,128]{3,2,1,0:T(8,128)}) custom-call(s32[4]{0:T(128)} %pad_add_fusion.place, f32[2,2048,256]{2,1,0:T(8,128)} %psi.3, f32[128,1024]{1,0:T(8,128)} %get-tuple-element.25.refs_0_, f32[128,1024]{1,0:T(8,128)} %copy-done.3, f32[64,1024]{1,0:T(8,128)} %copy-done.14, ...), custom_call_target="tpu_custom_call" | custom-call | flops 3221225472 | tf_op jit(solution)/shard_map/pallas_call | solution.py:62
  91.2 7.6 %all-to-all-start.1 = ((f32[8,8,16,128]{3,2,1,0:T(8,128)}), f32[8,8,16,128]{3,2,1,0:T(8,128)S(1)}, u32[]{:S(2)}, u32[]{:S(2)}) async-start(f32[8,8,16,128]{3,2,1,0:T(8,128)} %add.64), calls=%async_computation.1 | async-start | bytes 1048576 | tf_op jit(solution)/shard_map/all_to_all | solution.py:24
  100.7 9.3 %all-to-all-done.1 = f32[8,8,16,128]{3,2,1,0:T(8,128)S(1)} async-done(((f32[8,8,16,128]{3,2,1,0:T(8,128)}), f32[8,8,16,128]{3,2,1,0:T(8,128)S(1)}, u32[]{:S(2)}, u32[]{:S(2)}) %all-to-all-start.1) | async-done | bytes 524320 | tf_op jit(solution)/shard_map/all_to_all | solution.py:24
  110.0 3.5 %all-to-all-start = ((f32[8,8,16,128]{3,2,1,0:T(8,128)}), f32[8,8,16,128]{3,2,1,0:T(8,128)S(1)}, u32[]{:S(2)}, u32[]{:S(2)}) async-start(f32[8,8,16,128]{3,2,1,0:T(8,128)} %add.63), calls=%async_computation | async-start | bytes 1048576 | tf_op jit(solution)/shard_map/all_to_all | solution.py:24
  116.6 7.5 %all-to-all-done = f32[8,8,16,128]{3,2,1,0:T(8,128)S(1)} async-done(((f32[8,8,16,128]{3,2,1,0:T(8,128)}), f32[8,8,16,128]{3,2,1,0:T(8,128)S(1)}, u32[]{:S(2)}, u32[]{:S(2)}) %all-to-all-start) | async-done | bytes 524320 | tf_op jit(solution)/shard_map/all_to_all | solution.py:24
  124.4 18.7 %all_to_all.20 = f32[16,2,3,16,128]{4,3,2,1,0:T(8,128)S(1)} all-to-all(f32[16,2,3,16,128]{4,3,2,1,0:T(8,128)S(1)} %broadcast_in_dim.6), channel_id=1, replica_groups=mesh['x'=4,'zh'=2,'c'=2,'y'=4,'zl'=2] {'zl','x','zh'}, dimensions={0} | all-to-all | bytes 1572864 | tf_op jit(solution)/shard_map/all_to_all | solution.py:24
  143.8 3.5 %all-to-all-start.3 = ((f32[16,2,1,16,128]{4,3,1,2,0:T(8,128)}), f32[16,2,1,16,128]{4,3,1,2,0:T(8,128)S(1)}, u32[]{:S(2)}, u32[]{:S(2)}) async-start(f32[16,2,1,16,128]{4,3,1,2,0:T(8,128)} %broadcast_in_dim.8), calls=%async_computation.3 | async-start | bytes 524288 | tf_op jit(solution)/shard_map/all_to_all | solution.py:24
  147.5 8.6 %all-to-all-done.3 = f32[16,2,1,16,128]{4,3,1,2,0:T(8,128)S(1)} async-done(((f32[16,2,1,16,128]{4,3,1,2,0:T(8,128)}), f32[16,2,1,16,128]{4,3,1,2,0:T(8,128)S(1)}, u32[]{:S(2)}, u32[]{:S(2)}) %all-to-all-start.3) | async-done | bytes 262176 | tf_op jit(solution)/shard_map/all_to_all | solution.py:24
  156.1 5.2 %shard_map.55 = (bf16[1024,1024]{1,0:T(8,128)(2,1)}, bf16[1024,1024]{1,0:T(8,128)(2,1)}) custom-call(s32[4]{0:T(128)} %pad_add_fusion.place, f32[2,2048,256]{2,1,0:T(8,128)} %psi.3, f32[512,256]{1,0:T(8,128)} %copy-done.8, f32[512,256]{1,0:T(8,128)} %collective-permute-done.1.re1, f32[512,256]{1,0:T(8,128)} %collective-permute-done.2.im0, f32[512,256]{1,0:T(8,128)} %copy-done.1), custom_call_target="tpu_custom_call" | custom-call | flops 6291456 | tf_op jit(solution)/shard_map/pallas_call | solution.py:62
  162.0 5.8 %shard_map.62 = (f32[64,1024]{1,0:T(8,128)}, f32[64,1024]{1,0:T(8,128)}) custom-call(s32[4]{0:T(128)} %pad_add_fusion.place, bf16[1024,1024]{1,0:T(8,128)(2,1)} %get-tuple-element.23.high, bf16[1024,1024]{1,0:T(8,128)(2,1)} %get-tuple-element.24.low, f32[2,8,2,1,16,128]{5,4,3,2,1,0:T(8,128)} %bitcast.28, f32[2,8,2,1,16,128]{5,4,3,2,1,0:T(8,128)} %copy-done.6), custom_call_target="tpu_custom_call" | custom-call | flops 805306368 | tf_op jit(solution)/shard_map/pallas_call | solution.py:62
  168.2 2.9 %collective-permute-start.23 = (f32[64,1024]{1,0:T(8,128)}, f32[64,1024]{1,0:T(8,128)S(1)}, u32[]{:S(2)}, u32[]{:S(2)}) collective-permute-start(f32[64,1024]{1,0:T(8,128)} %get-tuple-element.37), channel_id=1, source_target_pairs={{0,6},{2,0},{4,2},{6,4},{1,7},{3,1},{5,3},{7,5},{8,14},{10,8},{12,... | collective-permute-start | bytes 786440 | tf_op jit(solution)/shard_map/ppermute | solution.py:20
  171.0 7.0 %collective-permute-done.22.up = f32[64,1024]{1,0:T(8,128)S(1)} collective-permute-done((f32[64,1024]{1,0:T(8,128)}, f32[64,1024]{1,0:T(8,128)S(1)}, u32[]{:S(2)}, u32[]{:S(2)}) %collective-permute-start.22) | collective-permute-done | bytes 262176 | tf_op jit(solution)/shard_map/ppermute | solution.py:20
  179.8 6.9 %shard_map.63 = (f32[128,1024]{1,0:T(8,128)}, f32[128,1024]{1,0:T(8,128)}, f32[128,1024]{1,0:T(8,128)}) custom-call(s32[4]{0:T(128)} %pad_add_fusion.place, bf16[1024,1024]{1,0:T(8,128)(2,1)} %get-tuple-element.23.high, bf16[1024,1024]{1,0:T(8,128)(2,1)} %get-tuple-element.24.low, f32[2,8,2,3,16,128]{5,4,3,2,1,0:T(8,128)} %bitcast.31, ...), custom_call_target="tpu_custom_call" | custom-call | flops 2415919104 | tf_op jit(solution)/shard_map/pallas_call | solution.py:62
  187.7 2.2 collective-permute-start.25
  189.9 5.9 %shard_map.60 = (f32[64,1024]{1,0:T(8,128)}, f32[64,1024]{1,0:T(8,128)}) custom-call(s32[4]{0:T(128)} %pad_add_fusion.place, bf16[1024,1024]{1,0:T(8,128)(2,1)} %get-tuple-element.23.high, bf16[1024,1024]{1,0:T(8,128)(2,1)} %get-tuple-element.24.low, f32[2,8,2,1,16,128]{5,4,3,2,1,0:T(8,128)} %bitcast.29, f32[2,8,2,1,16,128]{5,4,3,2,1,0:T(8,128)} %copy-done.6), custom_call_target="tpu_custom_call" | custom-call | flops 805306368 | tf_op jit(solution)/shard_map/pallas_call | solution.py:62
  195.8 3.2 %collective-permute-start.19 = (f32[64,1024]{1,0:T(8,128)}, f32[64,1024]{1,0:T(8,128)S(1)}, u32[]{:S(2)}, u32[]{:S(2)}) collective-permute-start(f32[64,1024]{1,0:T(8,128)} %get-tuple-element.32), channel_id=1, source_target_pairs={{0,6},{2,0},{4,2},{6,4},{1,7},{3,1},{5,3},{7,5},{8,14},{10,8},{12,... | collective-permute-start | bytes 786440 | tf_op jit(solution)/shard_map/ppermute | solution.py:20
  199.1 8.2 %collective-permute-done.18.up = f32[64,1024]{1,0:T(8,128)S(1)} collective-permute-done((f32[64,1024]{1,0:T(8,128)}, f32[64,1024]{1,0:T(8,128)S(1)}, u32[]{:S(2)}, u32[]{:S(2)}) %collective-permute-start.18) | collective-permute-done | bytes 262176 | tf_op jit(solution)/shard_map/ppermute | solution.py:20
  208.7 7.0 %shard_map.61 = (f32[128,1024]{1,0:T(8,128)}, f32[128,1024]{1,0:T(8,128)}, f32[128,1024]{1,0:T(8,128)}) custom-call(s32[4]{0:T(128)} %pad_add_fusion.place, bf16[1024,1024]{1,0:T(8,128)(2,1)} %get-tuple-element.23.high, bf16[1024,1024]{1,0:T(8,128)(2,1)} %get-tuple-element.24.low, f32[2,8,2,3,16,128]{5,4,3,2,1,0:T(8,128)} %bitcast.32, ...), custom_call_target="tpu_custom_call" | custom-call | flops 2415919104 | tf_op jit(solution)/shard_map/pallas_call | solution.py:62
  215.9 3.0 %collective-permute-start.21 = (f32[128,1024]{1,0:T(8,128)}, f32[128,1024]{1,0:T(8,128)S(1)}, u32[]{:S(2)}, u32[]{:S(2)}) collective-permute-start(f32[128,1024]{1,0:T(8,128)} %get-tuple-element.35), channel_id=1, source_target_pairs={{0,6},{2,0},{4,2},{6,4},{1,7},{3,1},{5,3},{7,5},{8,14},{10,8},{12,... | collective-permute-start | bytes 1572872 | tf_op jit(solution)/shard_map/ppermute | solution.py:20
  219.8 10.0 %collective-permute-done.20.q0 = f32[128,1024]{1,0:T(8,128)S(1)} collective-permute-done((f32[128,1024]{1,0:T(8,128)}, f32[128,1024]{1,0:T(8,128)S(1)}, u32[]{:S(2)}, u32[]{:S(2)}) %collective-permute-start.20) | collective-permute-done | bytes 524320 | tf_op jit(solution)/shard_map/ppermute | solution.py:20
  232.1 4.0 %shard_map.64 = f32[128,2048]{1,0:T(8,128)} custom-call(s32[4]{0:T(128)} %pad_add_fusion.place, f32[128,2048]{1,0:T(8,128)} %bitcast.26, f32[128,1024]{1,0:T(8,128)} %get-tuple-element.33.p0, f32[128,1024]{1,0:T(8,128)} %copy-done.9, f32[128,1024]{1,0:T(8,128)} %copy-done.10, f32[128,1024]{1,0:T(8,128)} %copy-done.12), custom_call_target="tpu_custom_call" | custom-call | tf_op jit(solution)/shard_map/pallas_call | solution.py:62
  (101 shorter events, 36.1 us)
Async XLA Ops:
  5.8 14.3 %collective-permute-start.8 = (f32[128,1024]{1,0:T(8,128)}, f32[128,1024]{1,0:T(8,128)}, u32[]{:S(2)}, u32[]{:S(2)}) collective-permute-start(f32[128,1024]{1,0:T(8,128)} %get-tuple-element.26), channel_id=1, source_target_pairs={{0,1},{1,0},{2,3},{3,2},{4,5},{5,4},{6,7},{7,6},{8,9},{9,8},{10,11... | collective-permute-start | bytes 1572872 | tf_op jit(solution)/shard_map/ppermute | solution.py:20
  7.9 19.6 %collective-permute-start.5 = (f32[128,1024]{1,0:T(8,128)}, f32[128,1024]{1,0:T(8,128)S(1)}, u32[]{:S(2)}, u32[]{:S(2)}) collective-permute-start(f32[128,1024]{1,0:T(8,128)} %get-tuple-element.25.refs_0_), channel_id=1, source_target_pairs={{0,2},{2,4},{4,6},{6,0},{1,3},{3,5},{5,7},{7,1},{8,10},{10,12},{12... | collective-permute-start | bytes 1572872 | tf_op jit(solution)/shard_map/ppermute | solution.py:20
  9.4 18.4 %collective-permute-start.4 = (f32[128,1024]{1,0:T(8,128)}, f32[128,1024]{1,0:T(8,128)S(1)}, u32[]{:S(2)}, u32[]{:S(2)}) collective-permute-start(f32[128,1024]{1,0:T(8,128)} %get-tuple-element.25.refs_0_), channel_id=1, source_target_pairs={{0,6},{2,0},{4,2},{6,4},{1,7},{3,1},{5,3},{7,5},{8,14},{10,8},{12,... | collective-permute-start | bytes 1572872 | tf_op jit(solution)/shard_map/ppermute | solution.py:20
  20.1 14.5 %collective-permute-start.10 = (f32[128,1024]{1,0:T(8,128)}, f32[128,1024]{1,0:T(8,128)S(1)}, u32[]{:S(2)}, u32[]{:S(2)}) collective-permute-start(f32[128,1024]{1,0:T(8,128)} %collective-permute-done.8.refs_5_), channel_id=1, source_target_pairs={{0,2},{2,4},{4,6},{6,0},{1,3},{3,5},{5,7},{7,1},{8,10},{10,12},{12... | collective-permute-start | bytes 1572872 | tf_op jit(solution)/shard_map/ppermute | solution.py:20
  24.1 12.9 %collective-permute-start.9 = (f32[128,1024]{1,0:T(8,128)}, f32[128,1024]{1,0:T(8,128)S(1)}, u32[]{:S(2)}, u32[]{:S(2)}) collective-permute-start(f32[128,1024]{1,0:T(8,128)} %collective-permute-done.8.refs_5_), channel_id=1, source_target_pairs={{0,6},{2,0},{4,2},{6,4},{1,7},{3,1},{5,3},{7,5},{8,14},{10,8},{12,... | collective-permute-start | bytes 1572872 | tf_op jit(solution)/shard_map/ppermute | solution.py:20
  25.8 14.8 %collective-permute-start = (f32[512,256]{1,0:T(8,128)S(1)}, f32[512,256]{1,0:T(8,128)S(1)}, u32[]{:S(2)}, u32[]{:S(2)}) collective-permute-start(f32[512,256]{1,0:T(8,128)S(1)} %get-tuple-element.44), channel_id=1, source_target_pairs={{0,1},{1,0},{2,3},{3,2},{4,5},{5,4},{6,7},{7,6},{8,9},{9,8},{10,11... | collective-permute-start | bytes 1572872 | tf_op jit(solution)/shard_map/ppermute | solution.py:20
  27.5 42.1 %copy-start.2 = (f32[128,1024]{1,0:T(8,128)}, f32[128,1024]{1,0:T(8,128)S(1)}, u32[]{:S(2)}) copy-start(f32[128,1024]{1,0:T(8,128)S(1)} %collective-permute-done.5.refs_4_) | copy-start | bytes 1572868
  27.5 24.4 %collective-permute-start.1 = (f32[512,256]{1,0:T(8,128)S(1)}, f32[512,256]{1,0:T(8,128)}, u32[]{:S(2)}, u32[]{:S(2)}) collective-permute-start(f32[512,256]{1,0:T(8,128)S(1)} %get-tuple-element.43), channel_id=1, source_target_pairs={{0,1},{1,0},{2,3},{3,2},{4,5},{5,4},{6,7},{7,6},{8,9},{9,8},{10,11... | collective-permute-start | bytes 1572872 | tf_op jit(solution)/shard_map/ppermute | solution.py:20
  27.8 41.8 %copy-start.3 = (f32[128,1024]{1,0:T(8,128)}, f32[128,1024]{1,0:T(8,128)S(1)}, u32[]{:S(2)}) copy-start(f32[128,1024]{1,0:T(8,128)S(1)} %collective-permute-done.4.refs_1_) | copy-start | bytes 1572868
  27.8 35.3 %collective-permute-start.2 = (f32[512,256]{1,0:T(8,128)S(1)}, f32[512,256]{1,0:T(8,128)}, u32[]{:S(2)}, u32[]{:S(2)}) collective-permute-start(f32[512,256]{1,0:T(8,128)S(1)} %get-tuple-element.42), channel_id=1, source_target_pairs={{0,1},{1,0},{2,3},{3,2},{4,5},{5,4},{6,7},{7,6},{8,9},{9,8},{10,11... | collective-permute-start | bytes 1572872 | tf_op jit(solution)/shard_map/ppermute | solution.py:20
  34.6 41.9 %collective-permute-start.3 = (f32[512,256]{1,0:T(8,128)}, f32[512,256]{1,0:T(8,128)S(1)}, u32[]{:S(2)}, u32[]{:S(2)}) collective-permute-start(f32[512,256]{1,0:T(8,128)} %get-tuple-element.41), channel_id=1, source_target_pairs={{0,1},{1,0},{2,3},{3,2},{4,5},{5,4},{6,7},{7,6},{8,9},{9,8},{10,11... | collective-permute-start | bytes 1572872 | tf_op jit(solution)/shard_map/ppermute | solution.py:20
  37.0 27.9 %collective-permute-start.6 = (f32[64,1024]{1,0:T(8,128)S(1)}, f32[64,1024]{1,0:T(8,128)S(1)}, u32[]{:S(2)}, u32[]{:S(2)}) collective-permute-start(f32[64,1024]{1,0:T(8,128)S(1)} %slice.28), channel_id=1, source_target_pairs={{0,2},{2,4},{4,6},{6,0},{1,3},{3,5},{5,7},{7,1},{8,10},{10,12},{12... | collective-permute-start | bytes 786440 | tf_op jit(solution)/shard_map/ppermute | solution.py:20
  40.6 24.4 %collective-permute-start.7 = (f32[64,1024]{1,0:T(8,128)S(1)}, f32[64,1024]{1,0:T(8,128)}, u32[]{:S(2)}, u32[]{:S(2)}) collective-permute-start(f32[64,1024]{1,0:T(8,128)S(1)} %slice.29), channel_id=1, source_target_pairs={{0,6},{2,0},{4,2},{6,4},{1,7},{3,1},{5,3},{7,5},{8,14},{10,8},{12,... | collective-permute-start | bytes 786440 | tf_op jit(solution)/shard_map/ppermute | solution.py:20
  51.9 13.1 %collective-permute-start.11 = (f32[64,1024]{1,0:T(8,128)S(1)}, f32[64,1024]{1,0:T(8,128)}, u32[]{:S(2)}, u32[]{:S(2)}) collective-permute-start(f32[64,1024]{1,0:T(8,128)S(1)} %slice.30), channel_id=1, source_target_pairs={{0,2},{2,4},{4,6},{6,0},{1,3},{3,5},{5,7},{7,1},{8,10},{10,12},{12... | collective-permute-start | bytes 786440 | tf_op jit(solution)/shard_map/ppermute | solution.py:20
  63.1 6.5 %collective-permute-start.12 = (f32[64,1024]{1,0:T(8,128)S(1)}, f32[64,1024]{1,0:T(8,128)}, u32[]{:S(2)}, u32[]{:S(2)}) collective-permute-start(f32[64,1024]{1,0:T(8,128)S(1)} %slice.31), channel_id=1, source_target_pairs={{0,6},{2,0},{4,2},{6,4},{1,7},{3,1},{5,3},{7,5},{8,14},{10,8},{12,... | collective-permute-start | bytes 786440 | tf_op jit(solution)/shard_map/ppermute | solution.py:20
  82.0 8.3 %collective-permute-start.14 = (f32[8,8,16,128]{3,2,1,0:T(8,128)}, f32[8,8,16,128]{3,2,1,0:T(8,128)S(1)}, u32[]{:S(2)}, u32[]{:S(2)}) collective-permute-start(f32[8,8,16,128]{3,2,1,0:T(8,128)} %get-tuple-element.30), channel_id=1, source_target_pairs={{0,8},{8,0},{1,9},{9,1},{2,10},{10,2},{3,11},{11,3},{4,12},{12,4},... | collective-permute-start | bytes 1572872 | tf_op jit(solution)/shard_map/ppermute | solution.py:20
  89.9 8.9 %collective-permute-start.13 = (f32[8,8,16,128]{3,2,1,0:T(8,128)}, f32[8,8,16,128]{3,2,1,0:T(8,128)S(1)}, u32[]{:S(2)}, u32[]{:S(2)}) collective-permute-start(f32[8,8,16,128]{3,2,1,0:T(8,128)} %get-tuple-element.28), channel_id=1, source_target_pairs={{0,8},{8,0},{1,9},{9,1},{2,10},{10,2},{3,11},{11,3},{4,12},{12,4},... | collective-permute-start | bytes 1572872 | tf_op jit(solution)/shard_map/ppermute | solution.py:20
  91.2 18.8 %all-to-all-start.1 = ((f32[8,8,16,128]{3,2,1,0:T(8,128)}), f32[8,8,16,128]{3,2,1,0:T(8,128)S(1)}, u32[]{:S(2)}, u32[]{:S(2)}) async-start(f32[8,8,16,128]{3,2,1,0:T(8,128)} %add.64), calls=%async_computation.1 | async-start | bytes 1048576 | tf_op jit(solution)/shard_map/all_to_all | solution.py:24
  110.0 14.2 %all-to-all-start = ((f32[8,8,16,128]{3,2,1,0:T(8,128)}), f32[8,8,16,128]{3,2,1,0:T(8,128)S(1)}, u32[]{:S(2)}, u32[]{:S(2)}) async-start(f32[8,8,16,128]{3,2,1,0:T(8,128)} %add.63), calls=%async_computation | async-start | bytes 1048576 | tf_op jit(solution)/shard_map/all_to_all | solution.py:24
  113.5 10.7 %collective-permute-start.15 = (f32[8,16,128]{2,1,0:T(8,128)S(1)}, f32[8,16,128]{2,1,0:T(8,128)S(1)}, u32[]{:S(2)}, u32[]{:S(2)}) collective-permute-start(f32[8,16,128]{2,1,0:T(8,128)S(1)} %reduce_sum.19), channel_id=1, source_target_pairs={{0,1},{1,0},{2,3},{3,2},{4,5},{5,4},{6,7},{7,6},{8,9},{9,8},{10,11... | collective-permute-start | bytes 196616 | tf_op jit(solution)/shard_map/ppermute | solution.py:20
  143.8 12.2 %all-to-all-start.3 = ((f32[16,2,1,16,128]{4,3,1,2,0:T(8,128)}), f32[16,2,1,16,128]{4,3,1,2,0:T(8,128)S(1)}, u32[]{:S(2)}, u32[]{:S(2)}) async-start(f32[16,2,1,16,128]{4,3,1,2,0:T(8,128)} %broadcast_in_dim.8), calls=%async_computation.3 | async-start | bytes 524288 | tf_op jit(solution)/shard_map/all_to_all | solution.py:24
  147.4 30.6 %collective-permute-start.16 = (f32[2,8,2,3,16,128]{5,4,3,2,1,0:T(8,128)S(1)}, f32[2,8,2,3,16,128]{5,4,3,2,1,0:T(8,128)S(1)}, u32[]{:S(2)}, u32[]{:S(2)}) collective-permute-start(f32[2,8,2,3,16,128]{5,4,3,2,1,0:T(8,128)S(1)} %bitcast.30), channel_id=1, source_target_pairs={{0,8},{8,0},{1,9},{9,1},{2,10},{10,2},{3,11},{11,3},{4,12},{12,4},... | collective-permute-start | bytes 2359304 | tf_op jit(solution)/shard_map/ppermute | solution.py:20
  156.1 5.2 %collective-permute-start.17 = (f32[2,8,2,1,16,128]{5,4,3,2,1,0:T(8,128)S(1)}, f32[2,8,2,1,16,128]{5,4,3,2,1,0:T(8,128)S(1)}, u32[]{:S(2)}, u32[]{:S(2)}) collective-permute-start(f32[2,8,2,1,16,128]{5,4,3,2,1,0:T(8,128)S(1)} %bitcast.27), channel_id=1, source_target_pairs={{0,8},{8,0},{1,9},{9,1},{2,10},{10,2},{3,11},{11,3},{4,12},{12,4},... | collective-permute-start | bytes 786440 | tf_op jit(solution)/shard_map/ppermute | solution.py:20
  167.8 10.2 %collective-permute-start.22 = (f32[64,1024]{1,0:T(8,128)}, f32[64,1024]{1,0:T(8,128)S(1)}, u32[]{:S(2)}, u32[]{:S(2)}) collective-permute-start(f32[64,1024]{1,0:T(8,128)} %get-tuple-element.36), channel_id=1, source_target_pairs={{0,2},{2,4},{4,6},{6,0},{1,3},{3,5},{5,7},{7,1},{8,10},{10,12},{12... | collective-permute-start | bytes 786440 | tf_op jit(solution)/shard_map/ppermute | solution.py:20
  168.2 9.8 %collective-permute-start.23 = (f32[64,1024]{1,0:T(8,128)}, f32[64,1024]{1,0:T(8,128)S(1)}, u32[]{:S(2)}, u32[]{:S(2)}) collective-permute-start(f32[64,1024]{1,0:T(8,128)} %get-tuple-element.37), channel_id=1, source_target_pairs={{0,6},{2,0},{4,2},{6,4},{1,7},{3,1},{5,3},{7,5},{8,14},{10,8},{12,... | collective-permute-start | bytes 786440 | tf_op jit(solution)/shard_map/ppermute | solution.py:20
  186.7 32.3 %collective-permute-start.24 = (f32[128,1024]{1,0:T(8,128)}, f32[128,1024]{1,0:T(8,128)S(1)}, u32[]{:S(2)}, u32[]{:S(2)}) collective-permute-start(f32[128,1024]{1,0:T(8,128)} %get-tuple-element.39), channel_id=1, source_target_pairs={{0,2},{2,4},{4,6},{6,0},{1,3},{3,5},{5,7},{7,1},{8,10},{10,12},{12... | collective-permute-start | bytes 1572872 | tf_op jit(solution)/shard_map/ppermute | solution.py:20
  187.7 31.2 %collective-permute-start.25 = (f32[128,1024]{1,0:T(8,128)}, f32[128,1024]{1,0:T(8,128)S(1)}, u32[]{:S(2)}, u32[]{:S(2)}) collective-permute-start(f32[128,1024]{1,0:T(8,128)} %get-tuple-element.40), channel_id=1, source_target_pairs={{0,6},{2,0},{4,2},{6,4},{1,7},{3,1},{5,3},{7,5},{8,14},{10,8},{12,... | collective-permute-start | bytes 1572872 | tf_op jit(solution)/shard_map/ppermute | solution.py:20
  195.8 11.5 %collective-permute-start.18 = (f32[64,1024]{1,0:T(8,128)}, f32[64,1024]{1,0:T(8,128)S(1)}, u32[]{:S(2)}, u32[]{:S(2)}) collective-permute-start(f32[64,1024]{1,0:T(8,128)} %get-tuple-element.31), channel_id=1, source_target_pairs={{0,2},{2,4},{4,6},{6,0},{1,3},{3,5},{5,7},{7,1},{8,10},{10,12},{12... | collective-permute-start | bytes 786440 | tf_op jit(solution)/shard_map/ppermute | solution.py:20
  195.8 11.5 %collective-permute-start.19 = (f32[64,1024]{1,0:T(8,128)}, f32[64,1024]{1,0:T(8,128)S(1)}, u32[]{:S(2)}, u32[]{:S(2)}) collective-permute-start(f32[64,1024]{1,0:T(8,128)} %get-tuple-element.32), channel_id=1, source_target_pairs={{0,6},{2,0},{4,2},{6,4},{1,7},{3,1},{5,3},{7,5},{8,14},{10,8},{12,... | collective-permute-start | bytes 786440 | tf_op jit(solution)/shard_map/ppermute | solution.py:20
  215.7 14.1 %collective-permute-start.20 = (f32[128,1024]{1,0:T(8,128)}, f32[128,1024]{1,0:T(8,128)S(1)}, u32[]{:S(2)}, u32[]{:S(2)}) collective-permute-start(f32[128,1024]{1,0:T(8,128)} %get-tuple-element.34), channel_id=1, source_target_pairs={{0,2},{2,4},{4,6},{6,0},{1,3},{3,5},{5,7},{7,1},{8,10},{10,12},{12... | collective-permute-start | bytes 1572872 | tf_op jit(solution)/shard_map/ppermute | solution.py:20
  215.9 13.9 %collective-permute-start.21 = (f32[128,1024]{1,0:T(8,128)}, f32[128,1024]{1,0:T(8,128)S(1)}, u32[]{:S(2)}, u32[]{:S(2)}) collective-permute-start(f32[128,1024]{1,0:T(8,128)} %get-tuple-element.35), channel_id=1, source_target_pairs={{0,6},{2,0},{4,2},{6,4},{1,7},{3,1},{5,3},{7,5},{8,14},{10,8},{12,... | collective-permute-start | bytes 1572872 | tf_op jit(solution)/shard_map/ppermute | solution.py:20
  219.1 12.2 %collective-permute-start.26 = (f32[128,1024]{1,0:T(8,128)S(1)}, f32[128,1024]{1,0:T(8,128)S(1)}, u32[]{:S(2)}, u32[]{:S(2)}) collective-permute-start(f32[128,1024]{1,0:T(8,128)S(1)} %add_add_fusion), channel_id=1, source_target_pairs={{0,1},{1,0},{2,3},{3,2},{4,5},{5,4},{6,7},{7,6},{8,9},{9,8},{10,11... | collective-permute-start | bytes 1572872 | tf_op jit(solution)/shard_map/ppermute | solution.py:20
  (19 other events, 196.7 us)
where the time goes:
time: 237 us; the launch traced here: 236 us
  waiting for transfers between devices  94 us (40%)
  Pallas kernels  57.6 us (24%)
  starting transfers between devices  49.2 us (21%)
  blocking collectives  18.7 us (8%)
  local copies, waits for them, and re-layouts  11.5 us (5%)
  other arithmetic  3.56 us (2%)
    ppermute x27, waiting for transfers between devices, shifted(): return lax.ppermute(value, axis, [(i, (i + step) % n) for i in range(n)])  68.6 us
    pallas_call x10, Pallas kernels, call(): pl.pallas_call(kernel, grid_spec=pltpu.PrefetchScalarGridSpec(num_scalar_...  57.6 us
    ppermute x27, starting transfers between devices, shifted(): return lax.ppermute(value, axis, [(i, (i + step) % n) for i in range(n)])  34.6 us
    all_to_all x3, waiting for transfers between devices, traded(): return lax.all_to_all(value, axes, 0, 0, tiled=True)  25.4 us
    all_to_all x1, blocking collectives, traded(): return lax.all_to_all(value, axes, 0, 0, tiled=True)  18.7 us
    all_to_all x3, starting transfers between devices, traded(): return lax.all_to_all(value, axes, 0, 0, tiled=True)  14.6 us
    unnamed x42, local copies, waits for them, and re-layouts  5.52 us
  transfers between devices with their start and end apart: 30, of which 14 were waited for; matrix products, arithmetic and copies ran while one was open for 3% of the time, Pallas kernels for 16%

commit v1 on v0

v1 whole, which is shorter than its diff:
```python
import jax
import jax.numpy as jnp
from jax import lax
from jax.experimental import pallas as pl
from jax.experimental.pallas import tpu as pltpu
from jax.sharding import Mesh
from jax.sharding import PartitionSpec as P


PANEL = 128
LANES = 128
AXES = ("x", "zh", "c", "y", "zl")
REDUCE = ("x", "zh")
SPREAD = ("zl", "x", "zh")
CHUNKS = 4
F32 = jnp.float32


def shifted(value, axis, step):
    n = lax.axis_size(axis)
    return lax.ppermute(value, axis, [(i, (i + step) % n) for i in range(n)])


def traded(value, axes):
    return lax.all_to_all(value, axes, 0, 0, tiled=True)


def everyone(value, axes):
    return traded(jnp.broadcast_to(value[None], (lax.axis_size(axes), *value.shape)), axes)


def split(value):
    high = value.astype(jnp.bfloat16)
    low = (value - high.astype(F32)).astype(jnp.bfloat16)
    return high, low


def dot3(left, right, dims):
    (lh, ll), (rh, rl) = left, right

    def dot(a, b):
        return lax.dot_general(a, b, (dims, ((), ())), preferred_element_type=F32)

    return dot(lh, rh) + (dot(lh, rl) + dot(ll, rh))


def turned(value, block):
    half = block // 2
    pieces = []
    for k in range(0, value.shape[0], block):
        pieces += [value[k + half : k + block], -value[k : k + half]]
    return jnp.concatenate(pieces, axis=0)


def whole(value):
    zeros = (0,) * value.ndim
    return pl.BlockSpec(value.shape, lambda i, s: zeros)


def call(kernel, place, args, in_specs, out_shapes, flops=0, scratch=()):
    outs = [jax.ShapeDtypeStruct(s, d) for s, d in out_shapes]
    cost = pl.CostEstimate(flops=flops, bytes_accessed=0, transcendentals=0)
    return pl.pallas_call(
        kernel,
        grid_spec=pltpu.PrefetchScalarGridSpec(
            num_scalar_prefetch=1,
            grid=(1,),
            in_specs=in_specs,
            out_specs=[whole(o) for o in outs],
            scratch_shapes=list(scratch),
        ),
        out_shape=outs,
        cost_estimate=cost if flops else None,
    )(place, *args)


def rolled(place, which, ring, out):
    turn = place[which]
    tile = turn // LANES
    rest = turn % LANES
    lane = lax.broadcasted_iota(jnp.int32, (ring.shape[0], LANES), 1)

    def load(k):
        at = pl.multiple_of((tile + k) * LANES, LANES)
        return pltpu.roll(ring[:, pl.ds(at, LANES)], (LANES - rest) % LANES, 1)

    now = load(0)
    for k in range(ring.shape[1] // 2 // LANES):
        after = load(k + 1)
        out(k, jnp.where(lane < LANES - rest, now, after))
        now = after


def roll_kernel(place, stored, mine, other, ring):
    rows = stored.shape[1]
    ring[:, :rows] = stored[...]
    ring[:, rows : 2 * rows] = stored[...]
    tiles = rows // 2 // LANES

    def out(k, value):
        ref = mine if k < tiles else other
        at = k % tiles * LANES
        ref[:, at : at + LANES] = value

    rolled(place, 3, ring, out)


def finish_kernel(place, stored, p0, q0, r0, away, out, ring):
    half = away.shape[1]
    home = p0[...] + (q0[...] + r0[...])
    for k in (0, 2):
        ring[:, k * half : (k + 1) * half] = home
        ring[:, (k + 1) * half : (k + 2) * half] = away[...]

    def put(k, value):
        at = slice(k * LANES, (k + 1) * LANES)
        out[:, at] = stored[:, at] - value

    rolled(place, 2, ring, put)


def ready_own(place, psi, high, low):
    bands = psi.shape[2]
    for p in (0, 1):
        h, l = split(psi[p])
        high[:, p * bands : (p + 1) * bands] = h
        low[:, p * bands : (p + 1) * bands] = l


def ready_pair(place, re0, re1, im0, im1, high, low):
    part, bands = re0.shape
    for k, ref in enumerate((re0, re1, im0, im1)):
        h, l = split(ref[...])
        rows = slice(k % 2 * part, (k % 2 + 1) * part)
        high[rows, k // 2 * bands : (k // 2 + 1) * bands] = h
        low[rows, k // 2 * bands : (k // 2 + 1) * bands] = l


def put(place, total, cols, first, keep, send):
    bands = total.shape[1]
    left, right = total[:, : bands // 2], total[:, bands // 2 :]
    south = place[1] == 0
    shards, rows = keep.shape[0], keep.shape[2]
    for ref, value in ((keep, jnp.where(south, left, right)), (send, jnp.where(south, right, left))):
        for b in range(total.shape[0] // cols):
            for s in range(shards):
                at = b * cols + s * rows
                ref[s, first + b] = value[at : at + rows]


def own_kernel(place, psi_high, psi_low, *refs):
    blocks, (high, low, keep, send) = refs[:-4], refs[-4:]
    cols = blocks[0].shape[0]
    for group in (0, 1):
        base = (place[0] if group == 0 else 1 - place[0]) * (4 * cols)
        at = 0
        for ref in blocks[5 * group : 5 * group + 5]:
            h, l = split(ref[...])
            rows = pl.ds(pl.multiple_of(base + at, cols // 2), ref.shape[0])
            high[rows, :] = h
            low[rows, :] = l
            at += ref.shape[0]
    right = (psi_high[...], psi_low[...])
    step = 4 * cols
    bands = psi_high.shape[1] // 2
    for k in (0, 1):
        rows = slice(k * step, (k + 1) * step)
        both = dot3((high[rows], low[rows]), right, ((1,), (0,)))
        total = both[:, :bands] + turned(both[:, bands:], cols)
        put(place, total, cols, 4 * k, keep, send)


def pair_kernel(place, high, low, re0, re1, im0, out):
    part = im0.shape[0]
    cols = out.shape[0] // 8
    real = split(jnp.concatenate([re0[...], re1[...]], axis=0))
    imag = split(im0[...])
    step = 4 * cols
    for k in (0, 1):
        rows = slice(k * step, (k + 1) * step)
        total = dot3((high[rows], low[rows]), real, ((1,), (0,)))
        more = dot3((high[rows, :part], low[rows, :part]), imag, ((1,), (0,)))
        out[rows] = total + turned(more, cols)


def last_kernel(place, high, low, im1, before, keep, send):
    cols = before.shape[0] // 8
    imag = split(im1[...])
    step = 4 * cols
    for k in (0, 1):
        rows = slice(k * step, (k + 1) * step)
        more = dot3((high[rows], low[rows]), imag, ((1,), (0,)))
        put(place, before[rows] + turned(more, cols), cols, 4 * k, keep, send)


def set_weights(place, ref, other, half, base, w_high, w_low):
    zl, core = place[0], place[1]
    _, shards, _, blocks, rows, bands = ref.shape
    cols = shards * rows
    middle = cols // 2
    for which in (0, 1):
        offset = jnp.where(zl == which, 0, 4 * bands)
        for source, spot in ((ref, core), (other, 1 - core)):
            plain = pl.ds(pl.multiple_of(offset + spot * bands, bands), bands)
            cross = pl.ds(pl.multiple_of(offset + (2 + spot) * bands, bands), bands)
            for k in range(blocks):
                for s in range(shards):
                    h, l = split(source[which, s, half, k])
                    at = k * cols + s * rows
                    w_high[pl.ds(pl.multiple_of(base + at, rows), rows), plain] = h
                    w_low[pl.ds(pl.multiple_of(base + at, rows), rows), plain] = l
                    if s * rows < middle:
                        at += middle
                    else:
                        at, h, l = at - middle, -h, -l
                    w_high[pl.ds(pl.multiple_of(base + at, rows), rows), cross] = h
                    w_low[pl.ds(pl.multiple_of(base + at, rows), rows), cross] = l


def product(own_h, own_l, pair_h, pair_l, w_high, w_low, done):
    bands = own_h.shape[1]
    step = own_h.shape[0] // 2
    dims = ((1,), (1,))
    for k in (0, 1):
        rows = slice(k * step, (k + 1) * step)
        out = dot3((own_h[rows], own_l[rows]), (w_high[:, :bands], w_low[:, :bands]), dims)
        out += dot3((pair_h[rows], pair_l[rows]), (w_high[:, bands:], w_low[:, bands:]), dims)
        done(rows, out.T)


def far_kernel(place, oh, ol, ph, pl_, mine, other, pair_a, pair_b, own_a, own_b, w_high, w_low):
    cols = w_high.shape[0] // 2
    half = cols // 2
    for k in (0, 1):
        base = jnp.where(place[0] == k, cols, 0)
        set_weights(place, mine, other, k, base, w_high, w_low)

    def done(rows, out):
        for k, ref in enumerate((pair_a, pair_b, own_a, own_b)):
            ref[:, rows] = out[k * half : (k + 1) * half]

    product(oh, ol, ph, pl_, w_high, w_low, done)


def near_kernel(place, oh, ol, ph, pl_, mine, other, up, down, p0, to_next, to_prev, w_high, w_low):
    cols = p0.shape[0]
    half = cols // 2
    set_weights(place, mine, other, 0, 0, w_high, w_low)

    def done(rows, out):
        p0[:, rows] = out[:cols]
        to_next[:half, rows] = out[cols : cols + half] + up[:, rows]
        to_next[half:, rows] = out[cols + half : 2 * cols]
        to_prev[:half, rows] = out[2 * cols : 2 * cols + half]
        to_prev[half:, rows] = out[2 * cols + half :] + down[:, rows]

    product(oh, ol, ph, pl_, w_high, w_low, done)


def gather_y(block):
    half = block.shape[0] // 2
    before = shifted(block, "y", 1)
    after = shifted(block, "y", -1)
    far_a = shifted(before[:half], "y", 1)
    far_b = shifted(after[half:], "y", -1)
    return [block, after, far_a, far_b, before]


def per_device(psi, dpsi, band_weight, panel_band, slab_offset):
    zl, core = lax.axis_index("zl"), lax.axis_index("c")
    rows, nb = psi.shape[1:]
    half, cols = rows // 2, 2 * dpsi.shape[2]
    part = 2 * half // CHUNKS
    turn = slab_offset[lax.axis_index(("x", "zh", "c"))] + zl * half
    place = jnp.stack([zl, core, (2 * rows - turn) % rows, turn % rows]).astype(jnp.int32)
    stored = dpsi.swapaxes(1, 2).reshape(cols, rows)
    psi_spec = pl.BlockSpec((2, half, nb), lambda i, s: (0, s[0], 0))

    ring = [pltpu.VMEM((cols, 2 * rows + LANES), F32)]
    mine, other = call(
        roll_kernel, place, [stored], [whole(stored)], [((cols, half), F32)] * 2, scratch=ring
    )
    pair = shifted(other, "zl", 1)
    pieces = []
    for k in range(CHUNKS):
        plane, at = divmod(k * part, half)
        start = (plane, (1 - zl) * half + at, 0)
        piece = lax.dynamic_slice(psi, start, (1, part, nb))[0]
        pieces.append(shifted(piece, "zl", 1))
    blocks = gather_y(mine) + gather_y(pair)

    mac = 6 * 8 * cols * half
    b16 = [((half, 2 * nb), jnp.bfloat16)] * 2
    psi_own = call(ready_own, place, [psi], [psi_spec], b16, mac)
    shards = lax.axis_size(REDUCE)
    out = [((shards, 8, cols // shards, nb // 2), F32)] * 2
    args = [*psi_own, *blocks]
    shapes = [((8 * cols, half), jnp.bfloat16)] * 2 + out
    high, low, keep, send = call(own_kernel, place, args, [*map(whole, args)], shapes, mac * 2 * nb)
    over_c = keep + shifted(send, "c", 1)
    own_sum = traded(over_c, REDUCE).sum(0)

    args = [high, low, *pieces[:3]]
    shapes = [((8 * cols, nb), F32)]
    partial = call(pair_kernel, place, args, [*map(whole, args)], shapes, mac * nb * 3 // 2)[0]
    late = pl.BlockSpec((8 * cols, part), lambda i, s: (0, 1))
    args = [high, low, pieces[3], partial]
    specs = [late, late, whole(pieces[3]), whole(partial)]
    keep, send = call(last_kernel, place, args, specs, out, mac * nb // 2)
    over_c = keep + shifted(send, "c", 1)
    pair_sum = traded(over_c, REDUCE).sum(0)
    total = own_sum + shifted(pair_sum, "zl", 1)
    weight = lax.dynamic_slice_in_dim(band_weight, panel_band[core] * PANEL, PANEL)
    weighted = (total * weight).reshape(2, 4, cols // shards, nb // 2)

    psi_pair = call(ready_pair, place, pieces, [*map(whole, pieces)], b16, mac)
    far = weighted[:, 2:3]
    near = jnp.concatenate([weighted[:, :2], weighted[:, 3:]], axis=1)
    far_mine = everyone(far, SPREAD)
    far_mine = far_mine.reshape(2, shards, *far.shape)
    far_other = shifted(far_mine, "c", 1)
    near_mine = everyone(near, SPREAD)
    near_mine = near_mine.reshape(2, shards, *near.shape)
    near_other = shifted(near_mine, "c", 1)

    waves = [*psi_own, *psi_pair]
    args = [*waves, far_mine, far_other]
    shapes = [((cols // 2, half), F32)] * 4
    room = [pltpu.VMEM((2 * cols, 4 * nb), jnp.bfloat16)] * 2
    pa, pb, oa, ob = call(far_kernel, place, args, [*map(whole, args)], shapes, mac * nb, room)
    steps = [
        (shifted(pa, "y", 1), shifted(pb, "y", -1)), (shifted(oa, "y", 1), shifted(ob, "y", -1))
    ]
    results = []
    room = [pltpu.VMEM((3 * cols, 4 * nb), jnp.bfloat16)] * 2
    for which in (1, 0):
        up, down = steps[1 - which]
        args = [*waves, near_mine, near_other, up, down]

        def index(i, s, which=which):
            return (0, 0, 1 - s[0] if which else s[0], 0, 0, 0)

        near_spec = pl.BlockSpec((2, shards, 1, *near.shape[1:]), index)
        specs = [*map(whole, waves), near_spec, near_spec, whole(up), whole(down)]
        shapes = [((cols, half), F32)] * 3
        p0, to_next, to_prev = call(
            near_kernel, place, args, specs, shapes, mac * nb * 3 // 2, room
        )
        q0 = shifted(to_next, "y", 1)
        r0 = shifted(to_prev, "y", -1)
        results.append((p0, q0, r0))
    p0, q0, r0 = results[0]
    away = shifted(p0 + (q0 + r0), "zl", 1)
    args = [stored, *results[1], away]
    done = call(
        finish_kernel, place, args, [*map(whole, args)], [(stored.shape, F32)], scratch=ring
    )[0]
    return done.reshape(2, cols // 2, rows).swapaxes(1, 2)


def solution(mesh):
    fine = Mesh(mesh.devices.reshape(4, 2, 2, 4, 2), AXES)
    ga, ba = ("x", "zh", "c"), ("y", "zl")
    in_specs = (P(None, ga, ba), P(None, ga, ba), P(), P(ba), P())

    return jax.shard_map(
        per_device, mesh=fine, in_specs=in_specs, out_specs=P(None, ga, ba), check_vma=False
    )
```

time: 237 us -> 244 us (1.030)
  local copies, waits for them, and re-layouts: 11.5 us -> 15.6 us
  waiting for transfers between devices: 94 us -> 97.9 us
    unnamed x42 -> x54, local copies, waits for them, and re-layouts: 5.52 us -> 8.64 us
    ppermute x27, waiting for transfers between devices: 68.6 us -> 71.3 us  [shifted(): return lax.ppermute(value, axis, [(i, (i + step) % n) for i in range(n)])]
  transfers between devices with their start and end apart: 30 -> 30, of which waited for: 14 -> 12; matrix products, arithmetic and copies ran while one was open for 3% -> 3% of each run, Pallas kernels for 16% -> 15%
where the time goes in v1:
time: 244 us; the launch traced here: 243 us
  waiting for transfers between devices  97.9 us (40%)
  Pallas kernels  57.3 us (23%)
  starting transfers between devices  48.6 us (20%)
  blocking collectives  18.7 us (8%)
  local copies, waits for them, and re-layouts  15.6 us (6%)
  other arithmetic  3.65 us (1%)
    ppermute x27, waiting for transfers between devices, shifted(): return lax.ppermute(value, axis, [(i, (i + step) % n) for i in range(n)])  71.3 us
    pallas_call x10, Pallas kernels, call(): pl.pallas_call(kernel, grid_spec=pltpu.PrefetchScalarGridSpec(num_scalar_...  57.3 us
    ppermute x27, starting transfers between devices, shifted(): return lax.ppermute(value, axis, [(i, (i + step) % n) for i in range(n)])  34.1 us
    all_to_all x3, waiting for transfers between devices, traded(): return lax.all_to_all(value, axes, 0, 0, tiled=True)  26.5 us
    all_to_all x1, blocking collectives, traded(): return lax.all_to_all(value, axes, 0, 0, tiled=True)  18.7 us
    all_to_all x3, starting transfers between devices, traded(): return lax.all_to_all(value, axes, 0, 0, tiled=True)  14.5 us
    unnamed x54, local copies, waits for them, and re-layouts  8.64 us
  transfers between devices with their start and end apart: 30, of which 12 were waited for; matrix products, arithmetic and copies ran while one was open for 3% of the time, Pallas kernels for 15%

profile of v1, /device:TPU:0, one launch (start us, length us, event | category | flops | bytes accessed | tf_op | source)
XLA Modules:
  0.0 243.2 jit_solution(7790282315032575115)
XLA Ops:
  2.6 3.2 %shard_map.57 = (f32[128,1024]{1,0:T(8,128)}, f32[128,1024]{1,0:T(8,128)}) custom-call(s32[4]{0:T(128)} %pad_add_fusion.place, f32[128,2048]{1,0:T(8,128)} %bitcast.25), custom_call_target="tpu_custom_call" | custom-call | tf_op jit(solution)/shard_map/pallas_call | solution.py:63
  5.8 2.0 collective-permute-start.8
  11.1 8.9 %collective-permute-done.8.refs_5_ = f32[128,1024]{1,0:T(8,128)S(1)} collective-permute-done((f32[128,1024]{1,0:T(8,128)}, f32[128,1024]{1,0:T(8,128)S(1)}, u32[]{:S(2)}, u32[]{:S(2)}) %collective-permute-start.8) | collective-permute-done | bytes 524320 | tf_op jit(solution)/shard_map/ppermute | solution.py:21
  24.9 2.5 %collective-permute-start.7 = (f32[64,1024]{1,0:T(8,128)S(1)}, f32[64,1024]{1,0:T(8,128)S(1)}, u32[]{:S(2)}, u32[]{:S(2)}) collective-permute-start(f32[64,1024]{1,0:T(8,128)S(1)} %slice.29), channel_id=1, source_target_pairs={{0,6},{2,0},{4,2},{6,4},{1,7},{3,1},{5,3},{7,5},{8,14},{10,8},{12,... | collective-permute-start | bytes 786440 | tf_op jit(solution)/shard_map/ppermute | solution.py:21
  27.3 8.6 %collective-permute-done.10.refs_9_ = f32[128,1024]{1,0:T(8,128)S(1)} collective-permute-done((f32[128,1024]{1,0:T(8,128)S(1)}, f32[128,1024]{1,0:T(8,128)S(1)}, u32[]{:S(2)}, u32[]{:S(2)}) %collective-permute-start.10) | collective-permute-done | bytes 524320 | tf_op jit(solution)/shard_map/ppermute | solution.py:21
  37.1 2.9 %collective-permute-start.12 = (f32[64,1024]{1,0:T(8,128)S(1)}, f32[64,1024]{1,0:T(8,128)}, u32[]{:S(2)}, u32[]{:S(2)}) collective-permute-start(f32[64,1024]{1,0:T(8,128)S(1)} %slice.31), channel_id=1, source_target_pairs={{0,6},{2,0},{4,2},{6,4},{1,7},{3,1},{5,3},{7,5},{8,14},{10,8},{12,... | collective-permute-start | bytes 786440 | tf_op jit(solution)/shard_map/ppermute | solution.py:21
  40.1 2.7 %dynamic-slice_bitcast_fusion = (f32[512,256]{1,0:T(8,128)S(1)}, f32[512,256]{1,0:T(8,128)}, f32[512,256]{1,0:T(8,128)}, f32[512,256]{1,0:T(8,128)S(1)}) fusion(f32[2,2048,256]{2,1,0:T(8,128)} %psi.1, s32[]{:T(128)S(6)} %select_n.32, s32[]{:T(128)S(6)} %select_n.31), kind=kLoop, calls=%fused_computation.1 | loop fusion | bytes 4194312 | tf_op jit(solution)/shard_map/squeeze | solution.py:288
  47.3 3.8 %shard_map.55 = (bf16[1024,512]{1,0:T(8,128)(2,1)}, bf16[1024,512]{1,0:T(8,128)(2,1)}) custom-call(s32[4]{0:T(128)} %pad_add_fusion.place, f32[2,2048,256]{2,1,0:T(8,128)} %psi.1), custom_call_target="tpu_custom_call" | custom-call | flops 6291456 | tf_op jit(solution)/shard_map/pallas_call | solution.py:63
  51.8 8.7 %shard_map.58 = (bf16[1024,1024]{1,0:T(8,128)(2,1)}, bf16[1024,1024]{1,0:T(8,128)(2,1)}, f32[8,8,16,128]{3,2,1,0:T(8,128)}, f32[8,8,16,128]{3,2,1,0:T(8,128)}) custom-call(s32[4]{0:T(128)} %pad_add_fusion.place, bf16[1024,512]{1,0:T(8,128)(2,1)} %get-tuple-element.27.psi_high.oh, bf16[1024,512]{1,0:T(8,128)(2,1)} %get-tuple-element.28.psi_low.ol, ...), custom_call_target="tpu_custom_call" | custom-call | flops 3221225472 | tf_op jit(solution)/shard_map/pallas_call | solution.py:63
  60.4 8.5 %collective-permute-done.1.re1 = f32[512,256]{1,0:T(8,128)S(1)} collective-permute-done((f32[512,256]{1,0:T(8,128)}, f32[512,256]{1,0:T(8,128)S(1)}, u32[]{:S(2)}, u32[]{:S(2)}) %collective-permute-start.1) | collective-permute-done | bytes 524320 | tf_op jit(solution)/shard_map/ppermute | solution.py:21
  69.0 11.2 %collective-permute-done.2.im0 = f32[512,256]{1,0:T(8,128)S(1)} collective-permute-done((f32[512,256]{1,0:T(8,128)S(1)}, f32[512,256]{1,0:T(8,128)S(1)}, u32[]{:S(2)}, u32[]{:S(2)}) %collective-permute-start.2) | collective-permute-done | bytes 524320 | tf_op jit(solution)/shard_map/ppermute | solution.py:21
  81.1 6.9 %shard_map.59.before = f32[1024,256]{1,0:T(8,128)} custom-call(s32[4]{0:T(128)} %pad_add_fusion.place, bf16[1024,1024]{1,0:T(8,128)(2,1)} %get-tuple-element.35.high, bf16[1024,1024]{1,0:T(8,128)(2,1)} %get-tuple-element.36.low, f32[512,256]{1,0:T(8,128)} %copy-done.2, f32[512,256]{1,0:T(8,128)} %copy-done.3, f32[512,256]{1,0:T(8,128)} %copy-done.4), custom_call_target="tpu_custom_call" | custom-call | flops 2415919104 | tf_op jit(solution)/shard_map/pallas_call | solution.py:63
  88.8 4.6 %shard_map.60 = (f32[8,8,16,128]{3,2,1,0:T(8,128)}, f32[8,8,16,128]{3,2,1,0:T(8,128)}) custom-call(s32[4]{0:T(128)} %pad_add_fusion.place, bf16[1024,1024]{1,0:T(8,128)(2,1)} %get-tuple-element.35.high, bf16[1024,1024]{1,0:T(8,128)(2,1)} %get-tuple-element.36.low, f32[512,256]{1,0:T(8,128)} %copy-done, f32[1024,256]{1,0:T(8,128)} %shard_map.59.before), custom_call_target="tpu_custom_call" | custom-call | flops 805306368 | tf_op jit(solution)/shard_map/pallas_call | solution.py:63
  97.5 7.5 %all-to-all-start.1 = ((f32[8,8,16,128]{3,2,1,0:T(8,128)}), f32[8,8,16,128]{3,2,1,0:T(8,128)S(1)}, u32[]{:S(2)}, u32[]{:S(2)}) async-start(f32[8,8,16,128]{3,2,1,0:T(8,128)} %add.64), calls=%async_computation.1 | async-start | bytes 1048576 | tf_op jit(solution)/shard_map/all_to_all | solution.py:25
  105.9 10.3 %all-to-all-done.1 = f32[8,8,16,128]{3,2,1,0:T(8,128)S(1)} async-done(((f32[8,8,16,128]{3,2,1,0:T(8,128)}), f32[8,8,16,128]{3,2,1,0:T(8,128)S(1)}, u32[]{:S(2)}, u32[]{:S(2)}) %all-to-all-start.1) | async-done | bytes 524320 | tf_op jit(solution)/shard_map/all_to_all | solution.py:25
  116.2 3.5 %all-to-all-start = ((f32[8,8,16,128]{3,2,1,0:T(8,128)}), f32[8,8,16,128]{3,2,1,0:T(8,128)S(1)}, u32[]{:S(2)}, u32[]{:S(2)}) async-start(f32[8,8,16,128]{3,2,1,0:T(8,128)} %add.63), calls=%async_computation | async-start | bytes 1048576 | tf_op jit(solution)/shard_map/all_to_all | solution.py:25
  122.7 7.6 %all-to-all-done = f32[8,8,16,128]{3,2,1,0:T(8,128)S(1)} async-done(((f32[8,8,16,128]{3,2,1,0:T(8,128)}), f32[8,8,16,128]{3,2,1,0:T(8,128)S(1)}, u32[]{:S(2)}, u32[]{:S(2)}) %all-to-all-start) | async-done | bytes 524320 | tf_op jit(solution)/shard_map/all_to_all | solution.py:25
  130.5 18.7 %all_to_all.20 = f32[16,2,3,16,128]{4,3,2,1,0:T(8,128)S(1)} all-to-all(f32[16,2,3,16,128]{4,3,2,1,0:T(8,128)S(1)} %broadcast_in_dim.6), channel_id=1, replica_groups=mesh['x'=4,'zh'=2,'c'=2,'y'=4,'zl'=2] {'zl','x','zh'}, dimensions={0} | all-to-all | bytes 1572864 | tf_op jit(solution)/shard_map/all_to_all | solution.py:25
  150.0 3.5 %all-to-all-start.3 = ((f32[16,2,1,16,128]{4,3,1,2,0:T(8,128)}), f32[16,2,1,16,128]{4,3,1,2,0:T(8,128)S(1)}, u32[]{:S(2)}, u32[]{:S(2)}) async-start(f32[16,2,1,16,128]{4,3,1,2,0:T(8,128)} %broadcast_in_dim.8), calls=%async_computation.3 | async-start | bytes 524288 | tf_op jit(solution)/shard_map/all_to_all | solution.py:25
  153.6 8.6 %all-to-all-done.3 = f32[16,2,1,16,128]{4,3,1,2,0:T(8,128)S(1)} async-done(((f32[16,2,1,16,128]{4,3,1,2,0:T(8,128)}), f32[16,2,1,16,128]{4,3,1,2,0:T(8,128)S(1)}, u32[]{:S(2)}, u32[]{:S(2)}) %all-to-all-start.3) | async-done | bytes 262176 | tf_op jit(solution)/shard_map/all_to_all | solution.py:25
  162.2 3.9 %shard_map.56 = (bf16[1024,512]{1,0:T(8,128)(2,1)}, bf16[1024,512]{1,0:T(8,128)(2,1)}) custom-call(s32[4]{0:T(128)} %pad_add_fusion.place, f32[512,256]{1,0:T(8,128)} %copy-done.2, f32[512,256]{1,0:T(8,128)} %copy-done.3, f32[512,256]{1,0:T(8,128)} %copy-done.4, f32[512,256]{1,0:T(8,128)} %copy-done), custom_call_target="tpu_custom_call" | custom-call | flops 6291456 | tf_op jit(solution)/shard_map/pallas_call | solution.py:63
  166.8 6.1 %shard_map.61 = (f32[64,1024]{1,0:T(8,128)}, f32[64,1024]{1,0:T(8,128)}, f32[64,1024]{1,0:T(8,128)}, f32[64,1024]{1,0:T(8,128)}) custom-call(s32[4]{0:T(128)} %pad_add_fusion.place, bf16[1024,512]{1,0:T(8,128)(2,1)} %get-tuple-element.27.psi_high.oh, bf16[1024,512]{1,0:T(8,128)(2,1)} %get-tuple-element.28.psi_low.ol, ...), custom_call_target="tpu_custom_call" | custom-call | flops 1610612736 | tf_op jit(solution)/shard_map/pallas_call | solution.py:63
  173.0 3.2 %collective-permute-start.23 = (f32[64,1024]{1,0:T(8,128)}, f32[64,1024]{1,0:T(8,128)S(1)}, u32[]{:S(2)}, u32[]{:S(2)}) collective-permute-start(f32[64,1024]{1,0:T(8,128)} %get-tuple-element.45), channel_id=1, source_target_pairs={{0,6},{2,0},{4,2},{6,4},{1,7},{3,1},{5,3},{7,5},{8,14},{10,8},{12,... | collective-permute-start | bytes 786440 | tf_op jit(solution)/shard_map/ppermute | solution.py:21
  176.2 6.9 %collective-permute-done.22.up = f32[64,1024]{1,0:T(8,128)S(1)} collective-permute-done((f32[64,1024]{1,0:T(8,128)}, f32[64,1024]{1,0:T(8,128)S(1)}, u32[]{:S(2)}, u32[]{:S(2)}) %collective-permute-start.22) | collective-permute-done | bytes 262176 | tf_op jit(solution)/shard_map/ppermute | solution.py:21
  184.8 8.0 %shard_map.63 = (f32[128,1024]{1,0:T(8,128)}, f32[128,1024]{1,0:T(8,128)}, f32[128,1024]{1,0:T(8,128)}) custom-call(s32[4]{0:T(128)} %pad_add_fusion.place, bf16[1024,512]{1,0:T(8,128)(2,1)} %get-tuple-element.27.psi_high.oh, bf16[1024,512]{1,0:T(8,128)(2,1)} %get-tuple-element.28.psi_low.ol, bf16[1024,512]{1,0:T(8,128)(2,1)} %get-tuple-element.29.ph, ...), custom_call_target="tpu_custom_call" | custom-call | flops 2415919104 | tf_op jit(solution)/shard_map/pallas_call | solution.py:63
  192.9 3.2 %collective-permute-start.25 = (f32[128,1024]{1,0:T(8,128)}, f32[128,1024]{1,0:T(8,128)S(1)}, u32[]{:S(2)}, u32[]{:S(2)}) collective-permute-start(f32[128,1024]{1,0:T(8,128)} %get-tuple-element.48), channel_id=1, source_target_pairs={{0,6},{2,0},{4,2},{6,4},{1,7},{3,1},{5,3},{7,5},{8,14},{10,8},{12,... | collective-permute-start | bytes 1572872 | tf_op jit(solution)/shard_map/ppermute | solution.py:21
  196.1 3.2 %collective-permute-start.19 = (f32[64,1024]{1,0:T(8,128)S(1)}, f32[64,1024]{1,0:T(8,128)S(1)}, u32[]{:S(2)}, u32[]{:S(2)}) collective-permute-start(f32[64,1024]{1,0:T(8,128)S(1)} %copy-done.20), channel_id=1, source_target_pairs={{0,6},{2,0},{4,2},{6,4},{1,7},{3,1},{5,3},{7,5},{8,14},{10,8},{12,... | collective-permute-start | bytes 786440 | tf_op jit(solution)/shard_map/ppermute | solution.py:21
  199.3 14.0 %collective-permute-done.18.up = f32[64,1024]{1,0:T(8,128)S(1)} collective-permute-done((f32[64,1024]{1,0:T(8,128)}, f32[64,1024]{1,0:T(8,128)S(1)}, u32[]{:S(2)}, u32[]{:S(2)}) %collective-permute-start.18) | collective-permute-done | bytes 262176 | tf_op jit(solution)/shard_map/ppermute | solution.py:21
  214.8 8.1 %shard_map.62 = (f32[128,1024]{1,0:T(8,128)}, f32[128,1024]{1,0:T(8,128)}, f32[128,1024]{1,0:T(8,128)}) custom-call(s32[4]{0:T(128)} %pad_add_fusion.place, bf16[1024,512]{1,0:T(8,128)(2,1)} %get-tuple-element.27.psi_high.oh, bf16[1024,512]{1,0:T(8,128)(2,1)} %get-tuple-element.28.psi_low.ol, bf16[1024,512]{1,0:T(8,128)(2,1)} %get-tuple-element.29.ph, ...), custom_call_target="tpu_custom_call" | custom-call | flops 2415919104 | tf_op jit(solution)/shard_map/pallas_call | solution.py:63
  223.0 3.2 %collective-permute-start.21 = (f32[128,1024]{1,0:T(8,128)}, f32[128,1024]{1,0:T(8,128)S(1)}, u32[]{:S(2)}, u32[]{:S(2)}) collective-permute-start(f32[128,1024]{1,0:T(8,128)} %get-tuple-element.43), channel_id=1, source_target_pairs={{0,6},{2,0},{4,2},{6,4},{1,7},{3,1},{5,3},{7,5},{8,14},{10,8},{12,... | collective-permute-start | bytes 1572872 | tf_op jit(solution)/shard_map/ppermute | solution.py:21
  226.9 10.0 %collective-permute-done.20.q0 = f32[128,1024]{1,0:T(8,128)S(1)} collective-permute-done((f32[128,1024]{1,0:T(8,128)}, f32[128,1024]{1,0:T(8,128)S(1)}, u32[]{:S(2)}, u32[]{:S(2)}) %collective-permute-start.20) | collective-permute-done | bytes 524320 | tf_op jit(solution)/shard_map/ppermute | solution.py:21
  239.2 4.0 %shard_map.64 = f32[128,2048]{1,0:T(8,128)} custom-call(s32[4]{0:T(128)} %pad_add_fusion.place, f32[128,2048]{1,0:T(8,128)} %bitcast.26, f32[128,1024]{1,0:T(8,128)} %get-tuple-element.41.p0, f32[128,1024]{1,0:T(8,128)} %copy-done.6, f32[128,1024]{1,0:T(8,128)} %copy-done.7, f32[128,1024]{1,0:T(8,128)} %copy-done.8), custom_call_target="tpu_custom_call" | custom-call | tf_op jit(solution)/shard_map/pallas_call | solution.py:63
  (113 shorter events, 33.5 us)
Async XLA Ops:
  5.8 14.2 %collective-permute-start.8 = (f32[128,1024]{1,0:T(8,128)}, f32[128,1024]{1,0:T(8,128)S(1)}, u32[]{:S(2)}, u32[]{:S(2)}) collective-permute-start(f32[128,1024]{1,0:T(8,128)} %get-tuple-element.32), channel_id=1, source_target_pairs={{0,1},{1,0},{2,3},{3,2},{4,5},{5,4},{6,7},{7,6},{8,9},{9,8},{10,11... | collective-permute-start | bytes 1572872 | tf_op jit(solution)/shard_map/ppermute | solution.py:21
  7.8 15.4 %collective-permute-start.5 = (f32[128,1024]{1,0:T(8,128)}, f32[128,1024]{1,0:T(8,128)S(1)}, u32[]{:S(2)}, u32[]{:S(2)}) collective-permute-start(f32[128,1024]{1,0:T(8,128)} %get-tuple-element.31.refs_0_), channel_id=1, source_target_pairs={{0,2},{2,4},{4,6},{6,0},{1,3},{3,5},{5,7},{7,1},{8,10},{10,12},{12... | collective-permute-start | bytes 1572872 | tf_op jit(solution)/shard_map/ppermute | solution.py:21
  9.4 14.3 %collective-permute-start.4 = (f32[128,1024]{1,0:T(8,128)}, f32[128,1024]{1,0:T(8,128)S(1)}, u32[]{:S(2)}, u32[]{:S(2)}) collective-permute-start(f32[128,1024]{1,0:T(8,128)} %get-tuple-element.31.refs_0_), channel_id=1, source_target_pairs={{0,6},{2,0},{4,2},{6,4},{1,7},{3,1},{5,3},{7,5},{8,14},{10,8},{12,... | collective-permute-start | bytes 1572872 | tf_op jit(solution)/shard_map/ppermute | solution.py:21
  19.9 16.0 %collective-permute-start.10 = (f32[128,1024]{1,0:T(8,128)S(1)}, f32[128,1024]{1,0:T(8,128)S(1)}, u32[]{:S(2)}, u32[]{:S(2)}) collective-permute-start(f32[128,1024]{1,0:T(8,128)S(1)} %collective-permute-done.8.refs_5_), channel_id=1, source_target_pairs={{0,2},{2,4},{4,6},{6,0},{1,3},{3,5},{5,7},{7,1},{8,10},{10,12},{12... | collective-permute-start | bytes 1572872 | tf_op jit(solution)/shard_map/ppermute | solution.py:21
  21.5 15.6 %collective-permute-start.9 = (f32[128,1024]{1,0:T(8,128)S(1)}, f32[128,1024]{1,0:T(8,128)S(1)}, u32[]{:S(2)}, u32[]{:S(2)}) collective-permute-start(f32[128,1024]{1,0:T(8,128)S(1)} %collective-permute-done.8.refs_5_), channel_id=1, source_target_pairs={{0,6},{2,0},{4,2},{6,4},{1,7},{3,1},{5,3},{7,5},{8,14},{10,8},{12,... | collective-permute-start | bytes 1572872 | tf_op jit(solution)/shard_map/ppermute | solution.py:21
  23.2 21.3 %collective-permute-start.6 = (f32[64,1024]{1,0:T(8,128)S(1)}, f32[64,1024]{1,0:T(8,128)S(1)}, u32[]{:S(2)}, u32[]{:S(2)}) collective-permute-start(f32[64,1024]{1,0:T(8,128)S(1)} %slice.28), channel_id=1, source_target_pairs={{0,2},{2,4},{4,6},{6,0},{1,3},{3,5},{5,7},{7,1},{8,10},{10,12},{12... | collective-permute-start | bytes 786440 | tf_op jit(solution)/shard_map/ppermute | solution.py:21
  24.9 20.0 %collective-permute-start.7 = (f32[64,1024]{1,0:T(8,128)S(1)}, f32[64,1024]{1,0:T(8,128)S(1)}, u32[]{:S(2)}, u32[]{:S(2)}) collective-permute-start(f32[64,1024]{1,0:T(8,128)S(1)} %slice.29), channel_id=1, source_target_pairs={{0,6},{2,0},{4,2},{6,4},{1,7},{3,1},{5,3},{7,5},{8,14},{10,8},{12,... | collective-permute-start | bytes 786440 | tf_op jit(solution)/shard_map/ppermute | solution.py:21
  36.7 14.4 %collective-permute-start.11 = (f32[64,1024]{1,0:T(8,128)}, f32[64,1024]{1,0:T(8,128)}, u32[]{:S(2)}, u32[]{:S(2)}) collective-permute-start(f32[64,1024]{1,0:T(8,128)} %slice.30), channel_id=1, source_target_pairs={{0,2},{2,4},{4,6},{6,0},{1,3},{3,5},{5,7},{7,1},{8,10},{10,12},{12... | collective-permute-start | bytes 786440 | tf_op jit(solution)/shard_map/ppermute | solution.py:21
  37.1 14.6 %collective-permute-start.12 = (f32[64,1024]{1,0:T(8,128)S(1)}, f32[64,1024]{1,0:T(8,128)}, u32[]{:S(2)}, u32[]{:S(2)}) collective-permute-start(f32[64,1024]{1,0:T(8,128)S(1)} %slice.31), channel_id=1, source_target_pairs={{0,6},{2,0},{4,2},{6,4},{1,7},{3,1},{5,3},{7,5},{8,14},{10,8},{12,... | collective-permute-start | bytes 786440 | tf_op jit(solution)/shard_map/ppermute | solution.py:21
  42.8 17.7 %collective-permute-start = (f32[512,256]{1,0:T(8,128)}, f32[512,256]{1,0:T(8,128)S(1)}, u32[]{:S(2)}, u32[]{:S(2)}) collective-permute-start(f32[512,256]{1,0:T(8,128)} %get-tuple-element.51), channel_id=1, source_target_pairs={{0,1},{1,0},{2,3},{3,2},{4,5},{5,4},{6,7},{7,6},{8,9},{9,8},{10,11... | collective-permute-start | bytes 1572872 | tf_op jit(solution)/shard_map/ppermute | solution.py:21
  44.5 24.5 %collective-permute-start.1 = (f32[512,256]{1,0:T(8,128)}, f32[512,256]{1,0:T(8,128)S(1)}, u32[]{:S(2)}, u32[]{:S(2)}) collective-permute-start(f32[512,256]{1,0:T(8,128)} %get-tuple-element.50), channel_id=1, source_target_pairs={{0,1},{1,0},{2,3},{3,2},{4,5},{5,4},{6,7},{7,6},{8,9},{9,8},{10,11... | collective-permute-start | bytes 1572872 | tf_op jit(solution)/shard_map/ppermute | solution.py:21
  45.9 34.3 %collective-permute-start.2 = (f32[512,256]{1,0:T(8,128)S(1)}, f32[512,256]{1,0:T(8,128)S(1)}, u32[]{:S(2)}, u32[]{:S(2)}) collective-permute-start(f32[512,256]{1,0:T(8,128)S(1)} %get-tuple-element.52), channel_id=1, source_target_pairs={{0,1},{1,0},{2,3},{3,2},{4,5},{5,4},{6,7},{7,6},{8,9},{9,8},{10,11... | collective-permute-start | bytes 1572872 | tf_op jit(solution)/shard_map/ppermute | solution.py:21
  51.1 36.8 %collective-permute-start.3 = (f32[512,256]{1,0:T(8,128)S(1)}, f32[512,256]{1,0:T(8,128)S(1)}, u32[]{:S(2)}, u32[]{:S(2)}) collective-permute-start(f32[512,256]{1,0:T(8,128)S(1)} %get-tuple-element.49), channel_id=1, source_target_pairs={{0,1},{1,0},{2,3},{3,2},{4,5},{5,4},{6,7},{7,6},{8,9},{9,8},{10,11... | collective-permute-start | bytes 1572872 | tf_op jit(solution)/shard_map/ppermute | solution.py:21
  93.5 27.3 %copy-start.26 = (s32[2]{0:T(128)S(1)}, s32[2]{0:T(128)}, u32[]{:S(2)}) copy-start(s32[2]{0:T(128)} %param.8) | copy-start | bytes 28
  93.5 2.1 collective-permute-start.14
  93.5 11.5 %collective-permute-start.13 = (f32[8,8,16,128]{3,2,1,0:T(8,128)S(1)}, f32[8,8,16,128]{3,2,1,0:T(8,128)S(1)}, u32[]{:S(2)}, u32[]{:S(2)}) collective-permute-start(f32[8,8,16,128]{3,2,1,0:T(8,128)S(1)} %copy-done.17), channel_id=1, source_target_pairs={{0,8},{8,0},{1,9},{9,1},{2,10},{10,2},{3,11},{11,3},{4,12},{12,4},... | collective-permute-start | bytes 1572872 | tf_op jit(solution)/shard_map/ppermute | solution.py:21
  97.5 18.6 %all-to-all-start.1 = ((f32[8,8,16,128]{3,2,1,0:T(8,128)}), f32[8,8,16,128]{3,2,1,0:T(8,128)S(1)}, u32[]{:S(2)}, u32[]{:S(2)}) async-start(f32[8,8,16,128]{3,2,1,0:T(8,128)} %add.64), calls=%async_computation.1 | async-start | bytes 1048576 | tf_op jit(solution)/shard_map/all_to_all | solution.py:25
  116.2 14.2 %all-to-all-start = ((f32[8,8,16,128]{3,2,1,0:T(8,128)}), f32[8,8,16,128]{3,2,1,0:T(8,128)S(1)}, u32[]{:S(2)}, u32[]{:S(2)}) async-start(f32[8,8,16,128]{3,2,1,0:T(8,128)} %add.63), calls=%async_computation | async-start | bytes 1048576 | tf_op jit(solution)/shard_map/all_to_all | solution.py:25
  119.7 10.7 %collective-permute-start.15 = (f32[8,16,128]{2,1,0:T(8,128)S(1)}, f32[8,16,128]{2,1,0:T(8,128)S(1)}, u32[]{:S(2)}, u32[]{:S(2)}) collective-permute-start(f32[8,16,128]{2,1,0:T(8,128)S(1)} %reduce_sum.19), channel_id=1, source_target_pairs={{0,1},{1,0},{2,3},{3,2},{4,5},{5,4},{6,7},{7,6},{8,9},{9,8},{10,11... | collective-permute-start | bytes 196616 | tf_op jit(solution)/shard_map/ppermute | solution.py:21
  150.0 12.2 %all-to-all-start.3 = ((f32[16,2,1,16,128]{4,3,1,2,0:T(8,128)}), f32[16,2,1,16,128]{4,3,1,2,0:T(8,128)S(1)}, u32[]{:S(2)}, u32[]{:S(2)}) async-start(f32[16,2,1,16,128]{4,3,1,2,0:T(8,128)} %broadcast_in_dim.8), calls=%async_computation.3 | async-start | bytes 524288 | tf_op jit(solution)/shard_map/all_to_all | solution.py:25
  153.5 29.6 %collective-permute-start.16 = (f32[2,8,2,3,16,128]{5,4,3,2,1,0:T(8,128)S(1)}, f32[2,8,2,3,16,128]{5,4,3,2,1,0:T(8,128)S(1)}, u32[]{:S(2)}, u32[]{:S(2)}) collective-permute-start(f32[2,8,2,3,16,128]{5,4,3,2,1,0:T(8,128)S(1)} %bitcast.27), channel_id=1, source_target_pairs={{0,8},{8,0},{1,9},{9,1},{2,10},{10,2},{3,11},{11,3},{4,12},{12,4},... | collective-permute-start | bytes 2359304 | tf_op jit(solution)/shard_map/ppermute | solution.py:21
  162.2 3.9 %collective-permute-start.17 = (f32[2,8,2,1,16,128]{5,4,3,2,1,0:T(8,128)S(1)}, f32[2,8,2,1,16,128]{5,4,3,2,1,0:T(8,128)S(1)}, u32[]{:S(2)}, u32[]{:S(2)}) collective-permute-start(f32[2,8,2,1,16,128]{5,4,3,2,1,0:T(8,128)S(1)} %bitcast.32), channel_id=1, source_target_pairs={{0,8},{8,0},{1,9},{9,1},{2,10},{10,2},{3,11},{11,3},{4,12},{12,4},... | collective-permute-start | bytes 786440 | tf_op jit(solution)/shard_map/ppermute | solution.py:21
  173.0 10.1 %collective-permute-start.22 = (f32[64,1024]{1,0:T(8,128)}, f32[64,1024]{1,0:T(8,128)S(1)}, u32[]{:S(2)}, u32[]{:S(2)}) collective-permute-start(f32[64,1024]{1,0:T(8,128)} %get-tuple-element.44), channel_id=1, source_target_pairs={{0,2},{2,4},{4,6},{6,0},{1,3},{3,5},{5,7},{7,1},{8,10},{10,12},{12... | collective-permute-start | bytes 786440 | tf_op jit(solution)/shard_map/ppermute | solution.py:21
  173.0 10.1 %collective-permute-start.23 = (f32[64,1024]{1,0:T(8,128)}, f32[64,1024]{1,0:T(8,128)S(1)}, u32[]{:S(2)}, u32[]{:S(2)}) collective-permute-start(f32[64,1024]{1,0:T(8,128)} %get-tuple-element.45), channel_id=1, source_target_pairs={{0,6},{2,0},{4,2},{6,4},{1,7},{3,1},{5,3},{7,5},{8,14},{10,8},{12,... | collective-permute-start | bytes 786440 | tf_op jit(solution)/shard_map/ppermute | solution.py:21
  192.9 33.3 %collective-permute-start.24 = (f32[128,1024]{1,0:T(8,128)}, f32[128,1024]{1,0:T(8,128)S(1)}, u32[]{:S(2)}, u32[]{:S(2)}) collective-permute-start(f32[128,1024]{1,0:T(8,128)} %get-tuple-element.47), channel_id=1, source_target_pairs={{0,2},{2,4},{4,6},{6,0},{1,3},{3,5},{5,7},{7,1},{8,10},{10,12},{12... | collective-permute-start | bytes 1572872 | tf_op jit(solution)/shard_map/ppermute | solution.py:21
  192.9 33.3 %collective-permute-start.25 = (f32[128,1024]{1,0:T(8,128)}, f32[128,1024]{1,0:T(8,128)S(1)}, u32[]{:S(2)}, u32[]{:S(2)}) collective-permute-start(f32[128,1024]{1,0:T(8,128)} %get-tuple-element.48), channel_id=1, source_target_pairs={{0,6},{2,0},{4,2},{6,4},{1,7},{3,1},{5,3},{7,5},{8,14},{10,8},{12,... | collective-permute-start | bytes 1572872 | tf_op jit(solution)/shard_map/ppermute | solution.py:21
  196.1 17.3 %collective-permute-start.18 = (f32[64,1024]{1,0:T(8,128)}, f32[64,1024]{1,0:T(8,128)S(1)}, u32[]{:S(2)}, u32[]{:S(2)}) collective-permute-start(f32[64,1024]{1,0:T(8,128)} %get-tuple-element.39), channel_id=1, source_target_pairs={{0,2},{2,4},{4,6},{6,0},{1,3},{3,5},{5,7},{7,1},{8,10},{10,12},{12... | collective-permute-start | bytes 786440 | tf_op jit(solution)/shard_map/ppermute | solution.py:21
  196.1 30.1 %copy-start.9 = (f32[128,1024]{1,0:T(8,128)S(1)}, f32[128,1024]{1,0:T(8,128)}, u32[]{:S(2)}) copy-start(f32[128,1024]{1,0:T(8,128)} %get-tuple-element.46) | copy-start | bytes 1572868
  196.1 17.3 %collective-permute-start.19 = (f32[64,1024]{1,0:T(8,128)S(1)}, f32[64,1024]{1,0:T(8,128)S(1)}, u32[]{:S(2)}, u32[]{:S(2)}) collective-permute-start(f32[64,1024]{1,0:T(8,128)S(1)} %copy-done.20), channel_id=1, source_target_pairs={{0,6},{2,0},{4,2},{6,4},{1,7},{3,1},{5,3},{7,5},{8,14},{10,8},{12,... | collective-permute-start | bytes 786440 | tf_op jit(solution)/shard_map/ppermute | solution.py:21
  222.9 14.0 %collective-permute-start.20 = (f32[128,1024]{1,0:T(8,128)}, f32[128,1024]{1,0:T(8,128)S(1)}, u32[]{:S(2)}, u32[]{:S(2)}) collective-permute-start(f32[128,1024]{1,0:T(8,128)} %get-tuple-element.42), channel_id=1, source_target_pairs={{0,2},{2,4},{4,6},{6,0},{1,3},{3,5},{5,7},{7,1},{8,10},{10,12},{12... | collective-permute-start | bytes 1572872 | tf_op jit(solution)/shard_map/ppermute | solution.py:21
  223.0 14.0 %collective-permute-start.21 = (f32[128,1024]{1,0:T(8,128)}, f32[128,1024]{1,0:T(8,128)S(1)}, u32[]{:S(2)}, u32[]{:S(2)}) collective-permute-start(f32[128,1024]{1,0:T(8,128)} %get-tuple-element.43), channel_id=1, source_target_pairs={{0,6},{2,0},{4,2},{6,4},{1,7},{3,1},{5,3},{7,5},{8,14},{10,8},{12,... | collective-permute-start | bytes 1572872 | tf_op jit(solution)/shard_map/ppermute | solution.py:21
  226.3 12.1 %collective-permute-start.26 = (f32[128,1024]{1,0:T(8,128)S(1)}, f32[128,1024]{1,0:T(8,128)S(1)}, u32[]{:S(2)}, u32[]{:S(2)}) collective-permute-start(f32[128,1024]{1,0:T(8,128)S(1)} %add_add_fusion), channel_id=1, source_target_pairs={{0,1},{1,0},{2,3},{3,2},{4,5},{5,4},{6,7},{7,6},{8,9},{9,8},{10,11... | collective-permute-start | bytes 1572872 | tf_op jit(solution)/shard_map/ppermute | solution.py:21
  (25 other events, 148.8 us)

commit v2 on v1

--- a/solution.py
+++ b/solution.py
@@ -1,3 +1,5 @@
+from functools import partial as partial_of
+
 import jax
 import jax.numpy as jnp
 from jax import lax
@@ -52,25 +54,18 @@
     return jnp.concatenate(pieces, axis=0)
 
 
-def whole(value):
-    zeros = (0,) * value.ndim
-    return pl.BlockSpec(value.shape, lambda i, s: zeros)
-
-
-def call(kernel, place, args, in_specs, out_shapes, flops=0, scratch=()):
+def call(kernel, place, args, out_shapes, flops=0, scratch=(), limit=8):
     outs = [jax.ShapeDtypeStruct(s, d) for s, d in out_shapes]
     cost = pl.CostEstimate(flops=flops, bytes_accessed=0, transcendentals=0)
+    vmem = pl.BlockSpec(memory_space=pltpu.VMEM)
     return pl.pallas_call(
         kernel,
-        grid_spec=pltpu.PrefetchScalarGridSpec(
-            num_scalar_prefetch=1,
-            grid=(1,),
-            in_specs=in_specs,
-            out_specs=[whole(o) for o in outs],
-            scratch_shapes=list(scratch),
-        ),
+        in_specs=[pl.BlockSpec(memory_space=pltpu.SMEM)] + [vmem] * len(args),
+        out_specs=[vmem] * len(outs),
         out_shape=outs,
+        scratch_shapes=list(scratch),
         cost_estimate=cost if flops else None,
+        compiler_params=pltpu.CompilerParams(vmem_limit_bytes=limit * 2**20),
     )(place, *args)
 
 
@@ -120,9 +115,10 @@
 
 
 def ready_own(place, psi, high, low):
-    bands = psi.shape[2]
+    rows, bands = high.shape[0], psi.shape[2]
+    at = pl.multiple_of(place[0] * rows, rows)
     for p in (0, 1):
-        h, l = split(psi[p])
+        h, l = split(psi[p, pl.ds(at, rows), :])
         high[:, p * bands : (p + 1) * bands] = h
         low[:, p * bands : (p + 1) * bands] = l
 
@@ -184,12 +180,12 @@
 
 
 def last_kernel(place, high, low, im1, before, keep, send):
-    cols = before.shape[0] // 8
+    cols, part = before.shape[0] // 8, im1.shape[0]
     imag = split(im1[...])
     step = 4 * cols
     for k in (0, 1):
         rows = slice(k * step, (k + 1) * step)
-        more = dot3((high[rows], low[rows]), imag, ((1,), (0,)))
+        more = dot3((high[rows, part:], low[rows, part:]), imag, ((1,), (0,)))
         put(place, before[rows] + turned(more, cols), cols, 4 * k, keep, send)
 
 
@@ -242,10 +238,11 @@
     product(oh, ol, ph, pl_, w_high, w_low, done)
 
 
-def near_kernel(place, oh, ol, ph, pl_, mine, other, up, down, p0, to_next, to_prev, w_high, w_low):
+def near_kernel(which, place, oh, ol, ph, pl_, mine, other, up, down, p0, to_next, to_prev, w_high, w_low):
     cols = p0.shape[0]
     half = cols // 2
-    set_weights(place, mine, other, 0, 0, w_high, w_low)
+    column_half = 1 - place[0] if which else place[0]
+    set_weights(place, mine, other, column_half, 0, w_high, w_low)
 
     def done(rows, out):
         p0[:, rows] = out[:cols]
@@ -274,11 +271,10 @@
     turn = slab_offset[lax.axis_index(("x", "zh", "c"))] + zl * half
     place = jnp.stack([zl, core, (2 * rows - turn) % rows, turn % rows]).astype(jnp.int32)
     stored = dpsi.swapaxes(1, 2).reshape(cols, rows)
-    psi_spec = pl.BlockSpec((2, half, nb), lambda i, s: (0, s[0], 0))
 
     ring = [pltpu.VMEM((cols, 2 * rows + LANES), F32)]
     mine, other = call(
-        roll_kernel, place, [stored], [whole(stored)], [((cols, half), F32)] * 2, scratch=ring
+        roll_kernel, place, [stored], [((cols, half), F32)] * 2, scratch=ring
     )
     pair = shifted(other, "zl", 1)
     pieces = []
@@ -291,29 +287,27 @@
 
     mac = 6 * 8 * cols * half
     b16 = [((half, 2 * nb), jnp.bfloat16)] * 2
-    psi_own = call(ready_own, place, [psi], [psi_spec], b16, mac)
+    psi_own = call(ready_own, place, [psi], b16, mac)
     shards = lax.axis_size(REDUCE)
     out = [((shards, 8, cols // shards, nb // 2), F32)] * 2
     args = [*psi_own, *blocks]
     shapes = [((8 * cols, half), jnp.bfloat16)] * 2 + out
-    high, low, keep, send = call(own_kernel, place, args, [*map(whole, args)], shapes, mac * 2 * nb)
+    high, low, keep, send = call(own_kernel, place, args, shapes, mac * 2 * nb)
     over_c = keep + shifted(send, "c", 1)
     own_sum = traded(over_c, REDUCE).sum(0)
 
     args = [high, low, *pieces[:3]]
     shapes = [((8 * cols, nb), F32)]
-    partial = call(pair_kernel, place, args, [*map(whole, args)], shapes, mac * nb * 3 // 2)[0]
-    late = pl.BlockSpec((8 * cols, part), lambda i, s: (0, 1))
+    partial = call(pair_kernel, place, args, shapes, mac * nb * 3 // 2)[0]
     args = [high, low, pieces[3], partial]
-    specs = [late, late, whole(pieces[3]), whole(partial)]
-    keep, send = call(last_kernel, place, args, specs, out, mac * nb // 2)
+    keep, send = call(last_kernel, place, args, out, mac * nb // 2)
     over_c = keep + shifted(send, "c", 1)
     pair_sum = traded(over_c, REDUCE).sum(0)
     total = own_sum + shifted(pair_sum, "zl", 1)
     weight = lax.dynamic_slice_in_dim(band_weight, panel_band[core] * PANEL, PANEL)
     weighted = (total * weight).reshape(2, 4, cols // shards, nb // 2)
 
-    psi_pair = call(ready_pair, place, pieces, [*map(whole, pieces)], b16, mac)
+    psi_pair = call(ready_pair, place, pieces, b16, mac)
     far = weighted[:, 2:3]
     near = jnp.concatenate([weighted[:, :2], weighted[:, 3:]], axis=1)
     far_mine = everyone(far, SPREAD)
@@ -327,7 +321,7 @@
     args = [*waves, far_mine, far_other]
     shapes = [((cols // 2, half), F32)] * 4
     room = [pltpu.VMEM((2 * cols, 4 * nb), jnp.bfloat16)] * 2
-    pa, pb, oa, ob = call(far_kernel, place, args, [*map(whole, args)], shapes, mac * nb, room)
+    pa, pb, oa, ob = call(far_kernel, place, args, shapes, mac * nb, room)
     steps = [
         (shifted(pa, "y", 1), shifted(pb, "y", -1)), (shifted(oa, "y", 1), shifted(ob, "y", -1))
     ]
@@ -336,15 +330,9 @@
     for which in (1, 0):
         up, down = steps[1 - which]
         args = [*waves, near_mine, near_other, up, down]
-
-        def index(i, s, which=which):
-            return (0, 0, 1 - s[0] if which else s[0], 0, 0, 0)
-
-        near_spec = pl.BlockSpec((2, shards, 1, *near.shape[1:]), index)
-        specs = [*map(whole, waves), near_spec, near_spec, whole(up), whole(down)]
         shapes = [((cols, half), F32)] * 3
         p0, to_next, to_prev = call(
-            near_kernel, place, args, specs, shapes, mac * nb * 3 // 2, room
+            partial_of(near_kernel, which), place, args, shapes, mac * nb * 3 // 2, room
         )
         q0 = shifted(to_next, "y", 1)
         r0 = shifted(to_prev, "y", -1)
@@ -353,7 +341,7 @@
     away = shifted(p0 + (q0 + r0), "zl", 1)
     args = [stored, *results[1], away]
     done = call(
-        finish_kernel, place, args, [*map(whole, args)], [(stored.shape, F32)], scratch=ring
+        finish_kernel, place, args, [(stored.shape, F32)], scratch=ring
     )[0]
     return done.reshape(2, cols // 2, rows).swapaxes(1, 2)
 

time: 244 us -> 217 us (0.89)
  Pallas kernels: 57.3 us -> 27.6 us
    pallas_call x10, Pallas kernels: 57.3 us -> 27.6 us  [call(): pl.pallas_call(kernel, in_specs=[pl.BlockSpec(memory_space=pltpu.SMEM)] +...]
    ppermute x27, waiting for transfers between devices: 71.3 us -> 75.5 us  [shifted(): return lax.ppermute(value, axis, [(i, (i + step) % n) for i in range(n)])]
    unnamed x54 -> x46, local copies, waits for them, and re-layouts: 8.64 us -> 9 us
  transfers between devices with their start and end apart: 30 -> 30, of which waited for: 12 -> 15; matrix products, arithmetic and copies ran while one was open for 3% -> 4% of each run, Pallas kernels for 15% -> 8%
where the time goes in v2:
time: 217 us; the launch traced here: 216 us
  waiting for transfers between devices  99.9 us (46%)
  starting transfers between devices  49.2 us (23%)
  Pallas kernels  27.6 us (13%)
  blocking collectives  18.7 us (9%)
  local copies, waits for them, and re-layouts  14.8 us (7%)
  other arithmetic  4.13 us (2%)
    ppermute x27, waiting for transfers between devices, shifted(): return lax.ppermute(value, axis, [(i, (i + step) % n) for i in range(n)])  75.5 us
    ppermute x27, starting transfers between devices, shifted(): return lax.ppermute(value, axis, [(i, (i + step) % n) for i in range(n)])  35.2 us
    pallas_call x10, Pallas kernels, call(): pl.pallas_call(kernel, in_specs=[pl.BlockSpec(memory_space=pltpu.SMEM)] +...  27.6 us
    all_to_all x3, waiting for transfers between devices, traded(): return lax.all_to_all(value, axes, 0, 0, tiled=True)  24.4 us
    all_to_all x1, blocking collectives, traded(): return lax.all_to_all(value, axes, 0, 0, tiled=True)  18.7 us
    all_to_all x3, starting transfers between devices, traded(): return lax.all_to_all(value, axes, 0, 0, tiled=True)  14 us
    unnamed x46, local copies, waits for them, and re-layouts  9 us
  transfers between devices with their start and end apart: 30, of which 15 were waited for; matrix products, arithmetic and copies ran while one was open for 4% of the time, Pallas kernels for 8%

profile of v2, /device:TPU:0, one launch (start us, length us, event | category | flops | bytes accessed | tf_op | source)
XLA Modules:
  0.0 216.0 jit_solution(6253869826104776583)
XLA Ops:
  4.3 2.1 collective-permute-start.8
  8.0 1.7 collective-permute-start.4
  9.6 8.7 %collective-permute-done.8.refs_5_ = f32[128,1024]{1,0:T(8,128)S(1)} collective-permute-done((f32[128,1024]{1,0:T(8,128)S(1)}, f32[128,1024]{1,0:T(8,128)S(1)}, u32[]{:S(2)}, u32[]{:S(2)}) %collective-permute-start.8) | collective-permute-done | bytes 524320 | tf_op jit(solution)/shard_map/ppermute | solution.py:23
  19.9 1.7 collective-permute-start.9
  23.5 2.9 %collective-permute-start.7 = (f32[64,1024]{1,0:T(8,128)}, f32[64,1024]{1,0:T(8,128)S(1)}, u32[]{:S(2)}, u32[]{:S(2)}) collective-permute-start(f32[64,1024]{1,0:T(8,128)} %slice.29), channel_id=1, source_target_pairs={{0,6},{2,0},{4,2},{6,4},{1,7},{3,1},{5,3},{7,5},{8,14},{10,8},{12,... | collective-permute-start | bytes 786440 | tf_op jit(solution)/shard_map/ppermute | solution.py:23
  26.4 7.9 %collective-permute-done.10.refs_9_ = f32[128,1024]{1,0:T(8,128)S(1)} collective-permute-done((f32[128,1024]{1,0:T(8,128)S(1)}, f32[128,1024]{1,0:T(8,128)S(1)}, u32[]{:S(2)}, u32[]{:S(2)}) %collective-permute-start.10) | collective-permute-done | bytes 524320 | tf_op jit(solution)/shard_map/ppermute | solution.py:23
  34.8 2.9 %collective-permute-start.12 = (f32[64,1024]{1,0:T(8,128)S(1)}, f32[64,1024]{1,0:T(8,128)S(1)}, u32[]{:S(2)}, u32[]{:S(2)}) collective-permute-start(f32[64,1024]{1,0:T(8,128)S(1)} %slice.31), channel_id=1, source_target_pairs={{0,6},{2,0},{4,2},{6,4},{1,7},{3,1},{5,3},{7,5},{8,14},{10,8},{12,... | collective-permute-start | bytes 786440 | tf_op jit(solution)/shard_map/ppermute | solution.py:23
  39.4 1.8 collective-permute-start
  48.4 5.7 %shard_map.58 = (bf16[1024,1024]{1,0:T(8,128)(2,1)S(1)}, bf16[1024,1024]{1,0:T(8,128)(2,1)S(1)}, f32[8,8,16,128]{3,2,1,0:T(8,128)S(1)}, f32[8,8,16,128]{3,2,1,0:T(8,128)}) custom-call(s32[4]{0:T(128)S(1)} %pad_add_fusion.place, bf16[1024,512]{1,0:T(8,128)(2,1)S(1)} %get-tuple-element.27.psi_high.oh, bf16[1024,512]{1,0:T(8,128)(2,1)S(1)} %get-tuple-element.28.psi_low.ol, ...), custom_call_target="tpu_custom_call" | custom-call | flops 3221225472 | tf_op jit(solution)/shard_map/pallas_call | solution.py:61
  54.3 11.2 %collective-permute-done.1.re1 = f32[512,256]{1,0:T(8,128)S(1)} collective-permute-done((f32[512,256]{1,0:T(8,128)S(1)}, f32[512,256]{1,0:T(8,128)S(1)}, u32[]{:S(2)}, u32[]{:S(2)}) %collective-permute-start.1) | collective-permute-done | bytes 524320 | tf_op jit(solution)/shard_map/ppermute | solution.py:23
  65.5 11.2 %collective-permute-done.2.im0 = f32[512,256]{1,0:T(8,128)S(1)} collective-permute-done((f32[512,256]{1,0:T(8,128)S(1)}, f32[512,256]{1,0:T(8,128)S(1)}, u32[]{:S(2)}, u32[]{:S(2)}) %collective-permute-start.2) | collective-permute-done | bytes 524320 | tf_op jit(solution)/shard_map/ppermute | solution.py:23
  76.8 3.1 %shard_map.59.before = f32[1024,256]{1,0:T(8,128)S(1)} custom-call(s32[4]{0:T(128)S(1)} %pad_add_fusion.place, bf16[1024,1024]{1,0:T(8,128)(2,1)S(1)} %get-tuple-element.35.high, bf16[1024,1024]{1,0:T(8,128)(2,1)S(1)} %get-tuple-element.36.low, f32[512,256]{1,0:T(8,128)S(1)} %collective-permute-done.re0, f32[512,256]{1,0:T(8,128)S(1)} %collective-permute-done.1.re1, ...), custom_call_target="tpu_custom_call" | custom-call | flops 2415919104 | tf_op jit(solution)/shard_map/pallas_call | solution.py:61
  79.9 3.2 %collective-permute-done.3.im1 = f32[512,256]{1,0:T(8,128)S(1)} collective-permute-done((f32[512,256]{1,0:T(8,128)S(1)}, f32[512,256]{1,0:T(8,128)S(1)}, u32[]{:S(2)}, u32[]{:S(2)}) %collective-permute-start.3) | collective-permute-done | bytes 524320 | tf_op jit(solution)/shard_map/ppermute | solution.py:23
  87.6 7.0 %all-to-all-start.1 = ((f32[8,8,16,128]{3,2,1,0:T(8,128)}), f32[8,8,16,128]{3,2,1,0:T(8,128)S(1)}, u32[]{:S(2)}, u32[]{:S(2)}) async-start(f32[8,8,16,128]{3,2,1,0:T(8,128)} %add.64), calls=%async_computation.1 | async-start | bytes 1048576 | tf_op jit(solution)/shard_map/all_to_all | solution.py:27
  94.6 1.9 add.63
  96.5 9.2 %all-to-all-done.1 = f32[8,8,16,128]{3,2,1,0:T(8,128)S(1)} async-done(((f32[8,8,16,128]{3,2,1,0:T(8,128)}), f32[8,8,16,128]{3,2,1,0:T(8,128)S(1)}, u32[]{:S(2)}, u32[]{:S(2)}) %all-to-all-start.1) | async-done | bytes 524320 | tf_op jit(solution)/shard_map/all_to_all | solution.py:27
  106.6 3.5 %all-to-all-start = ((f32[8,8,16,128]{3,2,1,0:T(8,128)}), f32[8,8,16,128]{3,2,1,0:T(8,128)S(1)}, u32[]{:S(2)}, u32[]{:S(2)}) async-start(f32[8,8,16,128]{3,2,1,0:T(8,128)} %add.63), calls=%async_computation | async-start | bytes 1048576 | tf_op jit(solution)/shard_map/all_to_all | solution.py:27
  114.3 6.5 %all-to-all-done = f32[8,8,16,128]{3,2,1,0:T(8,128)S(1)} async-done(((f32[8,8,16,128]{3,2,1,0:T(8,128)}), f32[8,8,16,128]{3,2,1,0:T(8,128)S(1)}, u32[]{:S(2)}, u32[]{:S(2)}) %all-to-all-start) | async-done | bytes 524320 | tf_op jit(solution)/shard_map/all_to_all | solution.py:27
  121.0 18.7 %all_to_all.20 = f32[16,2,3,16,128]{4,3,2,1,0:T(8,128)S(1)} all-to-all(f32[16,2,3,16,128]{4,3,2,1,0:T(8,128)S(1)} %broadcast_in_dim.6), channel_id=1, replica_groups=mesh['x'=4,'zh'=2,'c'=2,'y'=4,'zl'=2] {'zl','x','zh'}, dimensions={0} | all-to-all | bytes 1572864 | tf_op jit(solution)/shard_map/all_to_all | solution.py:27
  140.4 3.5 %all-to-all-start.3 = ((f32[16,2,1,16,128]{4,3,1,2,0:T(8,128)}), f32[16,2,1,16,128]{4,3,1,2,0:T(8,128)S(1)}, u32[]{:S(2)}, u32[]{:S(2)}) async-start(f32[16,2,1,16,128]{4,3,1,2,0:T(8,128)} %broadcast_in_dim.8), calls=%async_computation.3 | async-start | bytes 524288 | tf_op jit(solution)/shard_map/all_to_all | solution.py:27
  144.0 8.6 %all-to-all-done.3 = f32[16,2,1,16,128]{4,3,1,2,0:T(8,128)S(1)} async-done(((f32[16,2,1,16,128]{4,3,1,2,0:T(8,128)}), f32[16,2,1,16,128]{4,3,1,2,0:T(8,128)S(1)}, u32[]{:S(2)}, u32[]{:S(2)}) %all-to-all-start.3) | async-done | bytes 262176 | tf_op jit(solution)/shard_map/all_to_all | solution.py:27
  156.6 2.8 %shard_map.61 = (f32[64,1024]{1,0:T(8,128)S(1)}, f32[64,1024]{1,0:T(8,128)S(1)}, f32[64,1024]{1,0:T(8,128)S(1)}, f32[64,1024]{1,0:T(8,128)S(1)}) custom-call(s32[4]{0:T(128)S(1)} %pad_add_fusion.place, bf16[1024,512]{1,0:T(8,128)(2,1)S(1)} %copy-done.10, bf16[1024,512]{1,0:T(8,128)(2,1)S(1)} %copy-done.12, bf16[1024,512]{1,0:T(8,128)(2,1)S(1)} %get-tuple-element.29.ph, ...), custom_call_target="tpu_custom_call" | custom-call | flops 1610612736 | tf_op jit(solution)/shard_map/pallas_call | solution.py:61
  159.5 3.2 %collective-permute-start.23 = (f32[64,1024]{1,0:T(8,128)S(1)}, f32[64,1024]{1,0:T(8,128)S(1)}, u32[]{:S(2)}, u32[]{:S(2)}) collective-permute-start(f32[64,1024]{1,0:T(8,128)S(1)} %get-tuple-element.45), channel_id=1, source_target_pairs={{0,6},{2,0},{4,2},{6,4},{1,7},{3,1},{5,3},{7,5},{8,14},{10,8},{12,... | collective-permute-start | bytes 786440 | tf_op jit(solution)/shard_map/ppermute | solution.py:23
  162.7 6.3 %collective-permute-done.22.up = f32[64,1024]{1,0:T(8,128)S(1)} collective-permute-done((f32[64,1024]{1,0:T(8,128)S(1)}, f32[64,1024]{1,0:T(8,128)S(1)}, u32[]{:S(2)}, u32[]{:S(2)}) %collective-permute-start.22) | collective-permute-done | bytes 262176 | tf_op jit(solution)/shard_map/ppermute | solution.py:23
  169.0 4.8 %shard_map.63 = (f32[128,1024]{1,0:T(8,128)S(1)}, f32[128,1024]{1,0:T(8,128)S(1)}, f32[128,1024]{1,0:T(8,128)S(1)}) custom-call(s32[4]{0:T(128)S(1)} %pad_add_fusion.place, bf16[1024,512]{1,0:T(8,128)(2,1)S(1)} %copy-done.10, bf16[1024,512]{1,0:T(8,128)(2,1)S(1)} %copy-done.12, bf16[1024,512]{1,0:T(8,128)(2,1)S(1)} %get-tuple-element.29.ph, ...), custom_call_target="tpu_custom_call" | custom-call | flops 2415919104 | tf_op jit(solution)/shard_map/pallas_call | solution.py:61
  174.0 3.2 %collective-permute-start.25 = (f32[128,1024]{1,0:T(8,128)S(1)}, f32[128,1024]{1,0:T(8,128)S(1)}, u32[]{:S(2)}, u32[]{:S(2)}) collective-permute-start(f32[128,1024]{1,0:T(8,128)S(1)} %get-tuple-element.48), channel_id=1, source_target_pairs={{0,6},{2,0},{4,2},{6,4},{1,7},{3,1},{5,3},{7,5},{8,14},{10,8},{12,... | collective-permute-start | bytes 1572872 | tf_op jit(solution)/shard_map/ppermute | solution.py:23
  177.2 3.2 %collective-permute-start.19 = (f32[64,1024]{1,0:T(8,128)S(1)}, f32[64,1024]{1,0:T(8,128)S(1)}, u32[]{:S(2)}, u32[]{:S(2)}) collective-permute-start(f32[64,1024]{1,0:T(8,128)S(1)} %get-tuple-element.40), channel_id=1, source_target_pairs={{0,6},{2,0},{4,2},{6,4},{1,7},{3,1},{5,3},{7,5},{8,14},{10,8},{12,... | collective-permute-start | bytes 786440 | tf_op jit(solution)/shard_map/ppermute | solution.py:23
  180.4 13.5 %collective-permute-done.18.up = f32[64,1024]{1,0:T(8,128)S(1)} collective-permute-done((f32[64,1024]{1,0:T(8,128)S(1)}, f32[64,1024]{1,0:T(8,128)S(1)}, u32[]{:S(2)}, u32[]{:S(2)}) %collective-permute-start.18) | collective-permute-done | bytes 262176 | tf_op jit(solution)/shard_map/ppermute | solution.py:23
  193.9 4.9 %shard_map.62 = (f32[128,1024]{1,0:T(8,128)S(1)}, f32[128,1024]{1,0:T(8,128)S(1)}, f32[128,1024]{1,0:T(8,128)S(1)}) custom-call(s32[4]{0:T(128)S(1)} %pad_add_fusion.place, bf16[1024,512]{1,0:T(8,128)(2,1)S(1)} %copy-done.10, bf16[1024,512]{1,0:T(8,128)(2,1)S(1)} %copy-done.12, bf16[1024,512]{1,0:T(8,128)(2,1)S(1)} %get-tuple-element.29.ph, ...), custom_call_target="tpu_custom_call" | custom-call | flops 2415919104 | tf_op jit(solution)/shard_map/pallas_call | solution.py:61
  199.7 2.4 %collective-permute-start.21 = (f32[128,1024]{1,0:T(8,128)S(1)}, f32[128,1024]{1,0:T(8,128)S(1)}, u32[]{:S(2)}, u32[]{:S(2)}) collective-permute-start(f32[128,1024]{1,0:T(8,128)S(1)} %get-tuple-element.43), channel_id=1, source_target_pairs={{0,6},{2,0},{4,2},{6,4},{1,7},{3,1},{5,3},{7,5},{8,14},{10,8},{12,... | collective-permute-start | bytes 1572872 | tf_op jit(solution)/shard_map/ppermute | solution.py:23
  202.9 9.4 %collective-permute-done.20.q0 = f32[128,1024]{1,0:T(8,128)S(1)} collective-permute-done((f32[128,1024]{1,0:T(8,128)S(1)}, f32[128,1024]{1,0:T(8,128)S(1)}, u32[]{:S(2)}, u32[]{:S(2)}) %collective-permute-start.20) | collective-permute-done | bytes 524320 | tf_op jit(solution)/shard_map/ppermute | solution.py:23
  214.0 2.1 shard_map.64
  (105 shorter events, 35.3 us)
Async XLA Ops:
  4.3 35.1 %copy-start.13 = (f32[128,1024]{1,0:T(8,128)}, f32[128,1024]{1,0:T(8,128)S(1)}, u32[]{:S(2)}) copy-start(f32[128,1024]{1,0:T(8,128)S(1)} %get-tuple-element.31.refs_0_) | copy-start | bytes 1572868
  4.3 14.0 %collective-permute-start.8 = (f32[128,1024]{1,0:T(8,128)S(1)}, f32[128,1024]{1,0:T(8,128)S(1)}, u32[]{:S(2)}, u32[]{:S(2)}) collective-permute-start(f32[128,1024]{1,0:T(8,128)S(1)} %get-tuple-element.32), channel_id=1, source_target_pairs={{0,1},{1,0},{2,3},{3,2},{4,5},{5,4},{6,7},{7,6},{8,9},{9,8},{10,11... | collective-permute-start | bytes 1572872 | tf_op jit(solution)/shard_map/ppermute | solution.py:23
  6.4 15.2 %collective-permute-start.5 = (f32[128,1024]{1,0:T(8,128)S(1)}, f32[128,1024]{1,0:T(8,128)S(1)}, u32[]{:S(2)}, u32[]{:S(2)}) collective-permute-start(f32[128,1024]{1,0:T(8,128)S(1)} %get-tuple-element.31.refs_0_), channel_id=1, source_target_pairs={{0,2},{2,4},{4,6},{6,0},{1,3},{3,5},{5,7},{7,1},{8,10},{10,12},{12... | collective-permute-start | bytes 1572872 | tf_op jit(solution)/shard_map/ppermute | solution.py:23
  8.0 14.0 %collective-permute-start.4 = (f32[128,1024]{1,0:T(8,128)S(1)}, f32[128,1024]{1,0:T(8,128)S(1)}, u32[]{:S(2)}, u32[]{:S(2)}) collective-permute-start(f32[128,1024]{1,0:T(8,128)S(1)} %get-tuple-element.31.refs_0_), channel_id=1, source_target_pairs={{0,6},{2,0},{4,2},{6,4},{1,7},{3,1},{5,3},{7,5},{8,14},{10,8},{12,... | collective-permute-start | bytes 1572872 | tf_op jit(solution)/shard_map/ppermute | solution.py:23
  18.3 16.0 %collective-permute-start.10 = (f32[128,1024]{1,0:T(8,128)S(1)}, f32[128,1024]{1,0:T(8,128)S(1)}, u32[]{:S(2)}, u32[]{:S(2)}) collective-permute-start(f32[128,1024]{1,0:T(8,128)S(1)} %collective-permute-done.8.refs_5_), channel_id=1, source_target_pairs={{0,2},{2,4},{4,6},{6,0},{1,3},{3,5},{5,7},{7,1},{8,10},{10,12},{12... | collective-permute-start | bytes 1572872 | tf_op jit(solution)/shard_map/ppermute | solution.py:23
  19.9 14.9 %collective-permute-start.9 = (f32[128,1024]{1,0:T(8,128)S(1)}, f32[128,1024]{1,0:T(8,128)S(1)}, u32[]{:S(2)}, u32[]{:S(2)}) collective-permute-start(f32[128,1024]{1,0:T(8,128)S(1)} %collective-permute-done.8.refs_5_), channel_id=1, source_target_pairs={{0,6},{2,0},{4,2},{6,4},{1,7},{3,1},{5,3},{7,5},{8,14},{10,8},{12,... | collective-permute-start | bytes 1572872 | tf_op jit(solution)/shard_map/ppermute | solution.py:23
  21.6 19.7 %collective-permute-start.6 = (f32[64,1024]{1,0:T(8,128)S(1)}, f32[64,1024]{1,0:T(8,128)S(1)}, u32[]{:S(2)}, u32[]{:S(2)}) collective-permute-start(f32[64,1024]{1,0:T(8,128)S(1)} %slice.28), channel_id=1, source_target_pairs={{0,2},{2,4},{4,6},{6,0},{1,3},{3,5},{5,7},{7,1},{8,10},{10,12},{12... | collective-permute-start | bytes 786440 | tf_op jit(solution)/shard_map/ppermute | solution.py:23
  23.5 18.9 %collective-permute-start.7 = (f32[64,1024]{1,0:T(8,128)}, f32[64,1024]{1,0:T(8,128)S(1)}, u32[]{:S(2)}, u32[]{:S(2)}) collective-permute-start(f32[64,1024]{1,0:T(8,128)} %slice.29), channel_id=1, source_target_pairs={{0,6},{2,0},{4,2},{6,4},{1,7},{3,1},{5,3},{7,5},{8,14},{10,8},{12,... | collective-permute-start | bytes 786440 | tf_op jit(solution)/shard_map/ppermute | solution.py:23
  34.3 11.3 %collective-permute-start.11 = (f32[64,1024]{1,0:T(8,128)S(1)}, f32[64,1024]{1,0:T(8,128)S(1)}, u32[]{:S(2)}, u32[]{:S(2)}) collective-permute-start(f32[64,1024]{1,0:T(8,128)S(1)} %slice.30), channel_id=1, source_target_pairs={{0,2},{2,4},{4,6},{6,0},{1,3},{3,5},{5,7},{7,1},{8,10},{10,12},{12... | collective-permute-start | bytes 786440 | tf_op jit(solution)/shard_map/ppermute | solution.py:23
  34.8 11.3 %collective-permute-start.12 = (f32[64,1024]{1,0:T(8,128)S(1)}, f32[64,1024]{1,0:T(8,128)S(1)}, u32[]{:S(2)}, u32[]{:S(2)}) collective-permute-start(f32[64,1024]{1,0:T(8,128)S(1)} %slice.31), channel_id=1, source_target_pairs={{0,6},{2,0},{4,2},{6,4},{1,7},{3,1},{5,3},{7,5},{8,14},{10,8},{12,... | collective-permute-start | bytes 786440 | tf_op jit(solution)/shard_map/ppermute | solution.py:23
  39.4 14.9 %collective-permute-start = (f32[512,256]{1,0:T(8,128)S(1)}, f32[512,256]{1,0:T(8,128)S(1)}, u32[]{:S(2)}, u32[]{:S(2)}) collective-permute-start(f32[512,256]{1,0:T(8,128)S(1)} %get-tuple-element.51), channel_id=1, source_target_pairs={{0,1},{1,0},{2,3},{3,2},{4,5},{5,4},{6,7},{7,6},{8,9},{9,8},{10,11... | collective-permute-start | bytes 1572872 | tf_op jit(solution)/shard_map/ppermute | solution.py:23
  42.0 23.6 %collective-permute-start.1 = (f32[512,256]{1,0:T(8,128)S(1)}, f32[512,256]{1,0:T(8,128)S(1)}, u32[]{:S(2)}, u32[]{:S(2)}) collective-permute-start(f32[512,256]{1,0:T(8,128)S(1)} %get-tuple-element.50), channel_id=1, source_target_pairs={{0,1},{1,0},{2,3},{3,2},{4,5},{5,4},{6,7},{7,6},{8,9},{9,8},{10,11... | collective-permute-start | bytes 1572872 | tf_op jit(solution)/shard_map/ppermute | solution.py:23
  43.1 33.7 %collective-permute-start.2 = (f32[512,256]{1,0:T(8,128)S(1)}, f32[512,256]{1,0:T(8,128)S(1)}, u32[]{:S(2)}, u32[]{:S(2)}) collective-permute-start(f32[512,256]{1,0:T(8,128)S(1)} %get-tuple-element.52), channel_id=1, source_target_pairs={{0,1},{1,0},{2,3},{3,2},{4,5},{5,4},{6,7},{7,6},{8,9},{9,8},{10,11... | collective-permute-start | bytes 1572872 | tf_op jit(solution)/shard_map/ppermute | solution.py:23
  45.6 37.6 %collective-permute-start.3 = (f32[512,256]{1,0:T(8,128)S(1)}, f32[512,256]{1,0:T(8,128)S(1)}, u32[]{:S(2)}, u32[]{:S(2)}) collective-permute-start(f32[512,256]{1,0:T(8,128)S(1)} %get-tuple-element.49), channel_id=1, source_target_pairs={{0,1},{1,0},{2,3},{3,2},{4,5},{5,4},{6,7},{7,6},{8,9},{9,8},{10,11... | collective-permute-start | bytes 1572872 | tf_op jit(solution)/shard_map/ppermute | solution.py:23
  84.7 2.0 collective-permute-start.14
  84.8 9.8 %collective-permute-start.13 = (f32[8,8,16,128]{3,2,1,0:T(8,128)}, f32[8,8,16,128]{3,2,1,0:T(8,128)}, u32[]{:S(2)}, u32[]{:S(2)}) collective-permute-start(f32[8,8,16,128]{3,2,1,0:T(8,128)} %get-tuple-element.34), channel_id=1, source_target_pairs={{0,8},{8,0},{1,9},{9,1},{2,10},{10,2},{3,11},{11,3},{4,12},{12,4},... | collective-permute-start | bytes 1572872 | tf_op jit(solution)/shard_map/ppermute | solution.py:23
  87.6 18.2 %all-to-all-start.1 = ((f32[8,8,16,128]{3,2,1,0:T(8,128)}), f32[8,8,16,128]{3,2,1,0:T(8,128)S(1)}, u32[]{:S(2)}, u32[]{:S(2)}) async-start(f32[8,8,16,128]{3,2,1,0:T(8,128)} %add.64), calls=%async_computation.1 | async-start | bytes 1048576 | tf_op jit(solution)/shard_map/all_to_all | solution.py:27
  106.6 14.2 %all-to-all-start = ((f32[8,8,16,128]{3,2,1,0:T(8,128)}), f32[8,8,16,128]{3,2,1,0:T(8,128)S(1)}, u32[]{:S(2)}, u32[]{:S(2)}) async-start(f32[8,8,16,128]{3,2,1,0:T(8,128)} %add.63), calls=%async_computation | async-start | bytes 1048576 | tf_op jit(solution)/shard_map/all_to_all | solution.py:27
  111.2 9.6 %collective-permute-start.15 = (f32[8,16,128]{2,1,0:T(8,128)S(1)}, f32[8,16,128]{2,1,0:T(8,128)S(1)}, u32[]{:S(2)}, u32[]{:S(2)}) collective-permute-start(f32[8,16,128]{2,1,0:T(8,128)S(1)} %reduce_sum.19), channel_id=1, source_target_pairs={{0,1},{1,0},{2,3},{3,2},{4,5},{5,4},{6,7},{7,6},{8,9},{9,8},{10,11... | collective-permute-start | bytes 196616 | tf_op jit(solution)/shard_map/ppermute | solution.py:23
  140.4 12.2 %all-to-all-start.3 = ((f32[16,2,1,16,128]{4,3,1,2,0:T(8,128)}), f32[16,2,1,16,128]{4,3,1,2,0:T(8,128)S(1)}, u32[]{:S(2)}, u32[]{:S(2)}) async-start(f32[16,2,1,16,128]{4,3,1,2,0:T(8,128)} %broadcast_in_dim.8), calls=%async_computation.3 | async-start | bytes 524288 | tf_op jit(solution)/shard_map/all_to_all | solution.py:27
  143.9 25.1 %collective-permute-start.16 = (f32[2,8,2,3,16,128]{5,4,3,2,1,0:T(8,128)S(1)}, f32[2,8,2,3,16,128]{5,4,3,2,1,0:T(8,128)}, u32[]{:S(2)}, u32[]{:S(2)}) collective-permute-start(f32[2,8,2,3,16,128]{5,4,3,2,1,0:T(8,128)S(1)} %bitcast.27), channel_id=1, source_target_pairs={{0,8},{8,0},{1,9},{9,1},{2,10},{10,2},{3,11},{11,3},{4,12},{12,4},... | collective-permute-start | bytes 2359304 | tf_op jit(solution)/shard_map/ppermute | solution.py:23
  152.6 1.5 collective-permute-start.17
  159.4 9.6 %collective-permute-start.22 = (f32[64,1024]{1,0:T(8,128)S(1)}, f32[64,1024]{1,0:T(8,128)S(1)}, u32[]{:S(2)}, u32[]{:S(2)}) collective-permute-start(f32[64,1024]{1,0:T(8,128)S(1)} %get-tuple-element.44), channel_id=1, source_target_pairs={{0,2},{2,4},{4,6},{6,0},{1,3},{3,5},{5,7},{7,1},{8,10},{10,12},{12... | collective-permute-start | bytes 786440 | tf_op jit(solution)/shard_map/ppermute | solution.py:23
  159.5 9.6 %collective-permute-start.23 = (f32[64,1024]{1,0:T(8,128)S(1)}, f32[64,1024]{1,0:T(8,128)S(1)}, u32[]{:S(2)}, u32[]{:S(2)}) collective-permute-start(f32[64,1024]{1,0:T(8,128)S(1)} %get-tuple-element.45), channel_id=1, source_target_pairs={{0,6},{2,0},{4,2},{6,4},{1,7},{3,1},{5,3},{7,5},{8,14},{10,8},{12,... | collective-permute-start | bytes 786440 | tf_op jit(solution)/shard_map/ppermute | solution.py:23
  173.9 28.2 %collective-permute-start.24 = (f32[128,1024]{1,0:T(8,128)S(1)}, f32[128,1024]{1,0:T(8,128)S(1)}, u32[]{:S(2)}, u32[]{:S(2)}) collective-permute-start(f32[128,1024]{1,0:T(8,128)S(1)} %get-tuple-element.47), channel_id=1, source_target_pairs={{0,2},{2,4},{4,6},{6,0},{1,3},{3,5},{5,7},{7,1},{8,10},{10,12},{12... | collective-permute-start | bytes 1572872 | tf_op jit(solution)/shard_map/ppermute | solution.py:23
  174.0 28.1 %collective-permute-start.25 = (f32[128,1024]{1,0:T(8,128)S(1)}, f32[128,1024]{1,0:T(8,128)S(1)}, u32[]{:S(2)}, u32[]{:S(2)}) collective-permute-start(f32[128,1024]{1,0:T(8,128)S(1)} %get-tuple-element.48), channel_id=1, source_target_pairs={{0,6},{2,0},{4,2},{6,4},{1,7},{3,1},{5,3},{7,5},{8,14},{10,8},{12,... | collective-permute-start | bytes 1572872 | tf_op jit(solution)/shard_map/ppermute | solution.py:23
  177.2 16.7 %collective-permute-start.18 = (f32[64,1024]{1,0:T(8,128)S(1)}, f32[64,1024]{1,0:T(8,128)S(1)}, u32[]{:S(2)}, u32[]{:S(2)}) collective-permute-start(f32[64,1024]{1,0:T(8,128)S(1)} %get-tuple-element.39), channel_id=1, source_target_pairs={{0,2},{2,4},{4,6},{6,0},{1,3},{3,5},{5,7},{7,1},{8,10},{10,12},{12... | collective-permute-start | bytes 786440 | tf_op jit(solution)/shard_map/ppermute | solution.py:23
  177.2 36.8 %copy-start.2 = (f32[2,2048,64]{1,2,0:T(8,128)S(1)}, f32[2,2048,64]{1,2,0:T(8,128)}, u32[]{:S(2)}) copy-start(f32[2,2048,64]{1,2,0:T(8,128)} %param.6) | copy-start | bytes 3145732
  177.2 16.7 %collective-permute-start.19 = (f32[64,1024]{1,0:T(8,128)S(1)}, f32[64,1024]{1,0:T(8,128)S(1)}, u32[]{:S(2)}, u32[]{:S(2)}) collective-permute-start(f32[64,1024]{1,0:T(8,128)S(1)} %get-tuple-element.40), channel_id=1, source_target_pairs={{0,6},{2,0},{4,2},{6,4},{1,7},{3,1},{5,3},{7,5},{8,14},{10,8},{12,... | collective-permute-start | bytes 786440 | tf_op jit(solution)/shard_map/ppermute | solution.py:23
  198.8 13.5 %collective-permute-start.20 = (f32[128,1024]{1,0:T(8,128)S(1)}, f32[128,1024]{1,0:T(8,128)S(1)}, u32[]{:S(2)}, u32[]{:S(2)}) collective-permute-start(f32[128,1024]{1,0:T(8,128)S(1)} %get-tuple-element.42), channel_id=1, source_target_pairs={{0,2},{2,4},{4,6},{6,0},{1,3},{3,5},{5,7},{7,1},{8,10},{10,12},{12... | collective-permute-start | bytes 1572872 | tf_op jit(solution)/shard_map/ppermute | solution.py:23
  199.7 12.6 %collective-permute-start.21 = (f32[128,1024]{1,0:T(8,128)S(1)}, f32[128,1024]{1,0:T(8,128)S(1)}, u32[]{:S(2)}, u32[]{:S(2)}) collective-permute-start(f32[128,1024]{1,0:T(8,128)S(1)} %get-tuple-element.43), channel_id=1, source_target_pairs={{0,6},{2,0},{4,2},{6,4},{1,7},{3,1},{5,3},{7,5},{8,14},{10,8},{12,... | collective-permute-start | bytes 1572872 | tf_op jit(solution)/shard_map/ppermute | solution.py:23
  202.2 11.8 %collective-permute-start.26 = (f32[128,1024]{1,0:T(8,128)S(1)}, f32[128,1024]{1,0:T(8,128)S(1)}, u32[]{:S(2)}, u32[]{:S(2)}) collective-permute-start(f32[128,1024]{1,0:T(8,128)S(1)} %add_add_fusion), channel_id=1, source_target_pairs={{0,1},{1,0},{2,3},{3,2},{4,5},{5,4},{6,7},{7,6},{8,9},{9,8},{10,11... | collective-permute-start | bytes 1572872 | tf_op jit(solution)/shard_map/ppermute | solution.py:23
  (21 other events, 146.9 us)
